TPU v7x, 256 devices: a 2x2x32 block of a 4x8x32 slice. The times are simulated.
256 devices in a mesh: groups: 4 (over y, x), row: 64 (over z, core).
Axes of the slice: x: 2, y: 2, z: 32, core: 2. Of those that a mesh axis runs over, the one named last changes fastest.
The devices are a block of a 4x8x32 slice.
Arguments:
- latent: bfloat16 [16, 64, 128, 16], P('groups', None, 'row'), parts along dimension 0, may hold values from -16 to 16, as said below
- w_in: bfloat16 [3, 3, 3, 16, 384], replicated, may hold values from -0.3125 to 0.3125
- gain_one: float32 [384], replicated, may hold values from 0.25 to 1.75
- w_mid: bfloat16 [3, 3, 3, 384, 384], replicated, may hold values from -0.0625 to 0.0625
- gain_two: float32 [384], replicated, may hold values from 0.25 to 1.75
- w_up: bfloat16 [3, 3, 384, 192], replicated, may hold values from -0.109375 to 0.109375
- gain_three: float32 [192], replicated, may hold values from 0.25 to 1.75
- w_low: bfloat16 [3, 3, 3, 192, 96], replicated, may hold values from -0.078125 to 0.078125
- gain_four: float32 [96], replicated, may hold values from 0.25 to 1.75
- w_out: bfloat16 [3, 3, 3, 96, 3], replicated, may hold values from -0.125 to 0.125
Outputs:
- frames_rgb: float32 [16, 3, 128, 256], P('groups', None, 'row'), parts along dimension 0
There are 4 independent parts, one for each index of `groups`. A program takes and returns all parts, laid end to end along the dimension named above; an argument that names none is the same for every part. Nothing has to cross between parts.
Inputs may be any that keep to these rules, and one draw needn't show every extreme that they name: latent is real-valued.
All inputs are finite; a program needn't handle non-finite values.
Results may differ from a plain program's by a relative error of at most 0.0058.
Values may be sent and summed in bfloat16 or wider, within the bound.
No kernel may reach another device: no remote copies, remote signals or barrier semaphores. Data moves between devices by JAX's collectives and lax.ppermute only.
A program may use at most 128 MiB of HBM per device.

v0:
```python
import functools
import math

import jax
import jax.numpy as jnp
from jax import lax
from jax.experimental import pallas as pl
from jax.experimental.pallas import tpu as pltpu
from jax.sharding import Mesh
from jax.sharding import PartitionSpec as P

ROW = ("ri", "rj")
EPS = 1e-06
HALO = 4
F32 = jnp.float32
BF16 = jnp.bfloat16
NT = (((1,), (1,)), ((), ()))


def tile_kernel(tr, tc, h, w, frames, dims, *refs):
    c_lat, c_hi, c_mid, c_lo = dims
    (place, x, g1, g2, g3, g4, w_in, w_mid, w_up, w_low, w_out, out,
     win_v, wmid_v, wup_v, wlow_v, wout_v,
     xf, x9, wt, first, act1, a9, second, act2, b9, wc, act3, c9, wl, a4, wo, zs, sems) = refs
    s = tc + 2 * HALO
    r_first, r_mid, r_up, r_low = tr + 6, tr + 4, tr + 2, tr + 1
    row0, col0 = place[0], place[1]

    copies = [pltpu.make_async_copy(w_in, win_v, sems.at[0])]
    for a in range(3):
        dst = wmid_v.at[:, (2 - a) * c_hi : (3 - a) * c_hi]
        copies.append(pltpu.make_async_copy(w_mid.at[a], dst, sems.at[1 + a]))
    copies.append(pltpu.make_async_copy(w_up, wup_v, sems.at[4]))
    copies.append(pltpu.make_async_copy(w_low, wlow_v, sems.at[5]))
    copies.append(pltpu.make_async_copy(w_out, wout_v, sems.at[6]))
    for copy in copies:
        copy.start()

    def inside(rows, row_shift, col_shift):
        r = lax.broadcasted_iota(jnp.int32, (rows, s, 1), 0) + (row0 + row_shift)
        c = lax.broadcasted_iota(jnp.int32, (rows, s, 1), 1) + (col0 + col_shift)
        ok = (r >= 0) & (r < h) & (c >= 0) & (c < w)
        return jnp.where(ok, 1.0, 0.0).astype(F32)

    def rms_act(v, gain, channels, mask):
        total = jnp.sum(v * v, axis=-1, keepdims=True)
        scale = lax.rsqrt(total * (1.0 / channels) + EPS) * mask
        z = v * scale * gain
        return 0.5 * z * (1.0 + jnp.tanh(0.5 * z))

    k1 = 128
    xf[...] = jnp.zeros(xf.shape, F32)
    xf[0 : x.shape[0], :] = x[...].astype(F32)
    m1 = r_first * s
    for b in range(3):
        for e in range(3):
            tap = 3 * b + e
            x9[:, tap * k1 : (tap + 1) * k1] = xf[s * b + e : s * b + e + m1, :].astype(BF16)
    wt[...] = jnp.zeros(wt.shape, BF16)
    copies[0].wait()
    for b in range(3):
        for e in range(3):
            for ti in range(frames):
                for to in range(ti, min(frames, ti + 3)):
                    at = (3 * b + e) * k1 + ti * c_lat
                    wt[at : at + c_lat, to * c_hi : (to + 1) * c_hi] = win_v[ti - to + 2, b, e]
    for half in range(frames // 2):
        y = jnp.dot(x9[...], wt[:, half * 2 * c_hi : (half + 1) * 2 * c_hi], preferred_element_type=F32)
        first[2 * half] = y[:, :c_hi]
        first[2 * half + 1] = y[:, c_hi:]

    def norm_one(i, carry):
        t, r = i // r_first, i % r_first
        v = first[t, pl.ds(pl.multiple_of(r * s, 8), s), :].reshape(1, s, c_hi)
        y = rms_act(v, g1[...].reshape(1, 1, c_hi), c_hi, inside(1, r - 3, -3))
        act1[t, pl.ds(pl.multiple_of(r * s, 8), s), :] = y.reshape(s, c_hi)
        return carry

    lax.fori_loop(0, frames * r_first, norm_one, 0, unroll=2)
    for t in range(frames):
        act1[t, m1:, :] = jnp.zeros((act1.shape[1] - m1, c_hi), F32)

    m2 = r_mid * s

    def fill_mid(t, carry):
        for b in range(3):
            for e in range(3):
                tap = 3 * b + e
                a9[t, :, tap * c_hi : (tap + 1) * c_hi] = act1[t, s * b + e : s * b + e + m2, :].astype(BF16)
        second[t] = first[t, s + 1 : s + 1 + m2, :]
        return carry

    lax.fori_loop(0, frames, fill_mid, 0)
    for a in range(3):
        copies[1 + a].wait()
    for t in range(frames):
        for d in range(min(3, frames - t)):
            second[t + d] += jnp.dot(a9[t], wmid_v[:, d * c_hi : (d + 1) * c_hi], preferred_element_type=F32)

    def norm_two(i, carry):
        t, r = i // r_mid, i % r_mid
        v = second[t, pl.ds(pl.multiple_of(r * s, 8), s), :].reshape(1, s, c_hi)
        y = rms_act(v, g2[...].reshape(1, 1, c_hi), c_hi, inside(1, r - 2, -2))
        act2[t, pl.ds(pl.multiple_of(r * s, 8), s), :] = y.reshape(s, c_hi)
        return carry

    lax.fori_loop(0, frames * r_mid, norm_two, 0, unroll=2)
    for t in range(frames):
        act2[t, m2:, :] = jnp.zeros((act2.shape[1] - m2, c_hi), F32)

    m3 = r_up * s

    def fill_up(t, carry):
        for b in range(3):
            for e in range(3):
                tap = 3 * b + e
                b9[pl.ds(pl.multiple_of(t * m3, 16), m3), tap * c_hi : (tap + 1) * c_hi] = act2[t, s * b + e : s * b + e + m3, :].astype(BF16)
        return carry

    lax.fori_loop(0, frames, fill_up, 0)
    copies[4].wait()

    def pairs(k):
        return (k[0], k[1] + k[2]), (k[0] + k[1], k[2])

    def combine(i, carry):
        at = pl.ds(pl.multiple_of(i * 32, 32), 32)
        tap = [[wup_v[b, e, at, :].astype(F32) for e in range(3)] for b in range(3)]
        by_row = [pairs([tap[b][e] for b in range(3)]) for e in range(3)]
        for p in range(2):
            for bb in range(2):
                by_col = pairs([by_row[e][p][bb] for e in range(3)])
                for q in range(2):
                    for ee in range(2):
                        wc[p, q, bb, at, ee * c_hi : (ee + 1) * c_hi] = by_col[q][ee].astype(BF16)
        return carry

    lax.fori_loop(0, c_mid // 32, combine, 0)
    for p in range(2):
        for q in range(2):
            mask = inside(r_up, -1, -1)

            def up_pair(f, carry, p=p, q=q, mask=mask):
                rows = pl.ds(pl.multiple_of(f * 2 * m3, 16), 2 * m3)
                top, low = (3 * p + q) * c_hi, (3 * p + 3 + q) * c_hi
                y = lax.dot_general(b9[rows, top : top + 2 * c_hi], wc[p, q, 0], NT, preferred_element_type=F32)
                y = y + lax.dot_general(b9[rows, low : low + 2 * c_hi], wc[p, q, 1], NT, preferred_element_type=F32)
                y = rms_act(y.reshape(2, r_up, s, c_mid), g3[...].reshape(1, 1, 1, c_mid), c_mid, mask[None])
                y = y.reshape(2, m3, c_mid)
                act3[2 * p + q, f, 0:m3, :] = jnp.concatenate([y[0], y[1]], axis=-1)
                act3[2 * p + q, f, m3:, :] = jnp.zeros((act3.shape[2] - m3, 2 * c_mid), F32)
                return carry

            lax.fori_loop(0, frames // 2, up_pair, 0)

    m4 = c9.shape[1]
    kt = 2 * c_mid
    copies[5].wait()
    wl[...] = jnp.zeros(wl.shape, BF16)
    for b in range(3):
        for e in range(3):
            at = (3 * b + e) * kt
            for fi in range(2):
                for to in range(4):
                    a = fi - to + 2
                    if 0 <= a <= 2:
                        wl[at + fi * c_mid : at + (fi + 1) * c_mid, to * 128 : to * 128 + c_lo] = wlow_v[a, b, e]
    where_from = (((1, 0), (0, 1), (1, 1)), ((0, 0), (1, 0), (0, 1)))
    for p in range(2):
        for q in range(2):
            for f in range(2):
                for b in range(3):
                    for e in range(3):
                        (pp, dr), (qq, dc) = where_from[p][b], where_from[q][e]
                        tap = 3 * b + e
                        at = s * dr + dc
                        c9[f, :, tap * kt : (tap + 1) * kt] = act3[2 * pp + qq, f, at : at + m4, :].astype(BF16)
            z0 = jnp.dot(c9[0], wl[...], preferred_element_type=F32)
            z1 = jnp.dot(c9[1], wl[:, :256], preferred_element_type=F32) + z0[:, 256:]
            mask = inside(r_low, -p, -q)
            for t in range(frames):
                v = (z0 if t < 2 else z1)[: r_low * s, (t % 2) * 128 : (t % 2 + 1) * 128]
                y = rms_act(v.reshape(r_low, s, 128), g4[...].reshape(1, 1, 128), c_lo, mask)
                a4[2 * p + q, 0 : r_low * s, t * 128 : (t + 1) * 128] = y.reshape(r_low * s, 128).astype(BF16)
            a4[2 * p + q, r_low * s :, :] = jnp.zeros((a4.shape[1] - r_low * s, frames * 128), BF16)

    wo[...] = jnp.zeros(wo.shape, BF16)
    copies[6].wait()
    for ti in range(frames):
        for to in range(ti, min(frames, ti + 3)):
            wo[to * 32 : (to + 1) * 32, ti * 128 : ti * 128 + c_lo] = wout_v[ti - to + 2]
    for k in range(4):
        zs[k, 0:m4, :] = lax.dot_general(a4[k], wo[...], NT, preferred_element_type=F32)
    m5 = tr * s
    where_from = (((1, 0), (0, 0), (1, 1)), ((0, 0), (1, 1), (0, 1)))
    for p in range(2):
        for q in range(2):
            total = jnp.zeros((m5, 128), F32)
            for b in range(3):
                for e in range(3):
                    (pp, dr), (qq, dc) = where_from[p][b], where_from[q][e]
                    part = zs[2 * pp + qq, s * dr + dc : s * dr + dc + m5, :]
                    shift = 3 * (3 * b + e)
                    total = total + (pltpu.roll(part, 128 - shift, 1) if shift else part)
            out[2 * p + q] = total


def run_tile(place, x, g1, g2, g3, g4, w_in, w_mid, w_up, w_low, w_out, tr, tc, h, w, frames):
    c_lat, c_hi = w_in.shape[-2:]
    c_mid, c_lo = w_low.shape[-2:]
    s = tc + 2 * HALO
    m1, m2, m3, m5 = (tr + 6) * s, (tr + 4) * s, (tr + 2) * s, tr * s
    m4 = -(-(tr + 1) * s // 16) * 16
    vmem = pl.BlockSpec(memory_space=pltpu.VMEM)
    anywhere = pl.BlockSpec(memory_space=pl.ANY)
    scratch = [
        pltpu.VMEM(w_in.shape, BF16),
        pltpu.VMEM((9 * c_hi, 3 * c_hi), BF16),
        pltpu.VMEM(w_up.shape, BF16),
        pltpu.VMEM(w_low.shape, BF16),
        pltpu.VMEM(w_out.shape, BF16),
        pltpu.VMEM((m1 + 2 * s + 8, 128), F32),
        pltpu.VMEM((m1, 9 * 128), BF16),
        pltpu.VMEM((9 * 128, frames * c_hi), BF16),
        pltpu.VMEM((frames, m1, c_hi), F32),
        pltpu.VMEM((frames, m1 + 8, c_hi), F32),
        pltpu.VMEM((frames, m2, 9 * c_hi), BF16),
        pltpu.VMEM((frames, m2, c_hi), F32),
        pltpu.VMEM((frames, m2 + 8, c_hi), F32),
        pltpu.VMEM((frames * m3, 9 * c_hi), BF16),
        pltpu.VMEM((2, 2, 2, c_mid, 2 * c_hi), BF16),
        pltpu.VMEM((4, frames // 2, m3 + 16, 2 * c_mid), F32),
        pltpu.VMEM((2, m4, 18 * c_mid), BF16),
        pltpu.VMEM((18 * c_mid, 512), BF16),
        pltpu.VMEM((4, m4, frames * 128), BF16),
        pltpu.VMEM((128, frames * 128), BF16),
        pltpu.VMEM((4, m4 + 8, 128), F32),
        pltpu.SemaphoreType.DMA((7,)),
    ]
    return pl.pallas_call(
        functools.partial(tile_kernel, tr, tc, h, w, frames, (c_lat, c_hi, c_mid, c_lo)),
        out_shape=jax.ShapeDtypeStruct((4, m5, 128), F32),
        in_specs=[pl.BlockSpec(memory_space=pltpu.SMEM)] + [vmem] * 5 + [anywhere] * 5,
        out_specs=vmem,
        scratch_shapes=scratch,
        compiler_params=pltpu.CompilerParams(vmem_limit_bytes=56 * 1024 * 1024),
        name="tile",
    )(place, x, g1, g2, g3, g4, w_in, w_mid, w_up, w_low, w_out)


def gather_tile(latent, side, tr):
    frames, h, cols, ch = latent.shape
    lanes = frames * cols * ch
    mine = jnp.transpose(latent, (1, 2, 0, 3)).reshape(h, lanes)
    near = HALO // cols
    perm = []
    for g in range(side):
        for k in range(near):
            if g + 1 < side:
                perm.append((g * side + side - near + k, (g + 1) * side + k))
            if g > 0:
                perm.append((g * side + k, (g - 1) * side + side - near + k))
    beside = lax.ppermute(mine, ROW, perm)
    both = jnp.stack([mine, beside])
    tall = jnp.pad(both, ((0, 0), (HALO, HALO), (0, 0)))
    rows = tr + 2 * HALO
    blocks = jnp.stack([tall[:, tr * i : tr * i + rows] for i in range(side)])
    got = lax.all_to_all(blocks, "rj", 0, 0, tiled=True)
    pieces = jnp.concatenate([got[:near, 1], got[:, 0], got[side - near :, 1]])
    swap = [(side * a + b, side * b + a) for a in range(side) for b in range(side)]
    pieces = lax.ppermute(pieces, ROW, swap)
    tile = pieces.reshape(-1, rows, cols, frames * ch).transpose(1, 0, 2, 3)
    tile = tile.reshape(-1, frames * ch)
    return jnp.pad(tile, ((0, 0), (0, 128 - frames * ch)))


def per_device(latent, w_in, gain_one, w_mid, gain_two, w_up, gain_three, w_low, gain_four, w_out):
    frames, h, cols, _ = latent.shape
    side = lax.axis_size("ri")
    w = cols * side * side
    tr, tc = h // side, w // side
    s = tc + 2 * HALO
    x = gather_tile(latent, side, tr)
    place = jnp.stack([lax.axis_index("ri") * tr, lax.axis_index("rj") * tc]).astype(jnp.int32)
    c_lo, c_out = w_out.shape[-2:]
    colour = jnp.transpose(w_out, (0, 1, 2, 4, 3)).reshape(3, 9 * c_out, c_lo)
    colour = jnp.pad(colour, ((0, 0), (0, 32 - 9 * c_out), (0, 0)))
    out = run_tile(
        place, x, gain_one[None], gain_two[None], gain_three[None],
        jnp.pad(gain_four, (0, 128 - c_lo))[None], w_in,
        w_mid.reshape(3, -1, w_mid.shape[-1]), jnp.transpose(w_up, (0, 1, 3, 2)), w_low, colour,
        tr, tc, h, w, frames,
    )
    out = out.reshape(2, 2, tr, s, frames, 32)[:, :, :, :tc, :, :c_out]
    send = jnp.transpose(out, (2, 4, 5, 0, 3, 1)).reshape(tr, frames * c_out * 2, 2 * tc)
    got = lax.all_to_all(send, "rj", 0, 0, tiled=True)
    return jnp.transpose(got, (1, 0, 2)).reshape(frames, c_out, 2, 2 * w)


def solution(mesh):
    side = math.isqrt(mesh.shape["row"])
    grid = Mesh(mesh.devices.reshape(mesh.shape["groups"], side, side), ("groups",) + ROW)
    in_specs = (P("groups", None, ROW, None),) + (P(),) * 9
    out_specs = P("groups", None, ROW, None)
    return jax.shard_map(per_device, mesh=grid, in_specs=in_specs, out_specs=out_specs, check_vma=False)
```

profile of v0, /device:TPU:37, one launch (start us, length us, event | category | flops | bytes accessed | tf_op | source)
XLA Modules:
  0.0 111.6 jit_solution(1504716950940133039)
XLA Ops:
  0.0 0.0 copy-start.3
  0.0 0.0 copy-start
  0.0 0.0 copy-start.1
  0.0 0.0 copy-start.2
  0.0 0.8 copy.35
  0.8 0.7 collective-permute-start
  1.5 0.0 collective-permute-done
  1.5 0.2 fusion.11
  1.7 0.1 copy.39
  1.8 0.1 pad_slice_fusion.12
  1.9 0.1 copy.38
  2.0 0.6 constant_dynamic-update-slice_fusion.7
  2.6 0.1 copy.40
  2.7 0.1 copy.41
  2.7 0.1 copy.42
  2.8 0.1 copy.43
  2.9 0.1 copy.44
  3.0 0.1 copy.37
  3.1 0.6 constant_dynamic-update-slice_fusion.6
  3.7 0.6 constant_dynamic-update-slice_fusion.5
  4.3 0.6 constant_dynamic-update-slice_fusion.4
  4.9 0.6 constant_dynamic-update-slice_fusion.3
  5.5 0.6 constant_dynamic-update-slice_fusion.2
  6.1 0.6 constant_dynamic-update-slice_fusion.1
  6.7 0.6 constant_dynamic-update-slice_fusion
  7.3 23.7 %all-to-all-start = ((bf16[8,2,16,128]{3,2,1,0:T(8,128)(2,1)}), bf16[8,2,16,128]{3,2,1,0:T(8,128)(2,1)S(1)}, u32[]{:S(2)}, u32[]{:S(2)}) async-start(bf16[8,2,16,128]{3,2,1,0:T(8,128)(2,1)} %constant_dynamic-update-slice_fusion), calls=%async_computation | async-start | bytes 131072 | tf_op jit(solution)/shard_map/all_to_all | solution.py:268
  31.0 0.0 copy-done.3
  31.0 0.6 pad_bitcast_fusion.refs_5_
  31.5 4.6 %all-to-all-done = bf16[8,2,16,128]{3,2,1,0:T(8,128)(2,1)S(1)} async-done(((bf16[8,2,16,128]{3,2,1,0:T(8,128)(2,1)}), bf16[8,2,16,128]{3,2,1,0:T(8,128)(2,1)S(1)}, u32[]{:S(2)}, u32[]{:S(2)}) %all-to-all-start) | async-done | bytes 65568 | tf_op jit(solution)/shard_map/all_to_all | solution.py:268
  36.2 2.0 %collective-permute-start.1 = (bf16[12,16,128]{2,1,0:T(8,128)(2,1)S(1)}, bf16[12,16,128]{2,1,0:T(8,128)(2,1)S(1)}, u32[]{:S(2)}, u32[]{:S(2)}) collective-permute-start(bf16[12,16,128]{2,1,0:T(8,128)(2,1)S(1)} %pad_maximum_fusion.1), channel_id=1, source_target_pairs={{0,0},{1,8},{2,16},{3,24},{4,32},{5,40},{6,48},{7,56},{8,1},{9,9},... | collective-permute-start | bytes 147464 | tf_op jit(solution)/shard_map/ppermute | solution.py:271
  38.1 0.6 pad_add_fusion.refs_0_
  38.7 0.0 copy-done
  38.8 0.0 copy-done.1
  38.8 0.6 broadcast_in_dim.12.refs_2_
  39.4 0.0 copy-done.2
  39.4 0.5 broadcast_in_dim.13.refs_3_
  39.9 0.6 pad.19.refs_10_
  40.5 5.0 %collective-permute-done.1 = bf16[12,16,128]{2,1,0:T(8,128)(2,1)S(1)} collective-permute-done((bf16[12,16,128]{2,1,0:T(8,128)(2,1)S(1)}, bf16[12,16,128]{2,1,0:T(8,128)(2,1)S(1)}, u32[]{:S(2)}, u32[]{:S(2)}) %collective-permute-start.1) | collective-permute-done | bytes 49184 | tf_op jit(solution)/shard_map/ppermute | solution.py:271
  45.5 0.1 reshape.25
  45.6 0.1 copy.45
  45.7 0.7 pad.17.refs_1_
  46.3 38.3 %tile.1 = f32[4,192,128]{2,1,0:T(8,128)} custom-call(s32[2]{0:T(128)} %pad_add_fusion.refs_0_, bf16[384,128]{1,0:T(8,128)(2,1)} %pad.17.refs_1_, f32[1,384]{1,0:T(1,128)} %broadcast_in_dim.12.refs_2_, f32[1,384]{1,0:T(1,128)} %broadcast_in_dim.13.refs_3_, f32[1,192]{1,0:T(1,128)} %bitcast.53, f32[1,128]{1,0:T(1,128)} %pad_bitcast_fusion.refs_5_, ...), custom_call_target="tpu_custom_call" | custom-call | tf_op jit(solution)/shard_map/tile/pallas_call | solution.py:240
  84.6 1.7 %reshape.29 = f32[2,2,8,24,4,32]{5,4,3,2,1,0:T(4,128)S(1)} reshape(f32[4,192,128]{2,1,0:T(8,128)} %tile.1) | data formatting | bytes 786432 | tf_op jit(solution)/shard_map/reshape | solution.py:294
  86.3 0.1 slice.69
  86.4 1.9 %copy.49 = f32[2,2,8,16,4,3]{2,1,3,0,5,4:T(2,128)S(1)} copy(f32[2,2,8,16,4,3]{5,4,3,2,1,0:T(4,128)S(1)} %slice.69) | data formatting | bytes 49152
  88.3 0.2 copy.47
  88.5 0.1 reshape.32
  88.6 21.0 %all_to_all.10 = f32[8,1,768]{2,1,0:T(1,128)S(1)} all-to-all(f32[8,1,768]{2,1,0:T(1,128)S(1)} %reshape.32), channel_id=1, replica_groups=mesh['groups'=4,'ri'=8,'rj'=8] {'rj'}, dimensions={0} | all-to-all | bytes 49152 | tf_op jit(solution)/shard_map/all_to_all | solution.py:296
  109.5 0.5 broadcast.8
  110.0 0.7 reduce
  110.8 0.1 reshape.33
  110.9 0.7 reshape.31
  (6 shorter events, 0.1 us)
Async XLA Ops:
  0.0 31.0 %copy-start.3 = (f32[96]{0:T(128)S(1)}, f32[96]{0:T(128)}, u32[]{:S(2)}) copy-start(f32[96]{0:T(128)} %param.18) | copy-start | bytes 1156
  0.0 38.7 %copy-start = (bf16[3,3,3,96,3]{3,4,2,1,0:T(4,128)(2,1)S(1)}, bf16[3,3,3,96,3]{3,4,2,1,0:T(4,128)(2,1)}, u32[]{:S(2)}) copy-start(bf16[3,3,3,96,3]{3,4,2,1,0:T(4,128)(2,1)} %param.19) | copy-start | bytes 46660
  0.0 38.8 %copy-start.1 = (f32[384]{0:T(512)S(1)}, f32[384]{0:T(512)}, u32[]{:S(2)}) copy-start(f32[384]{0:T(512)} %param.12) | copy-start | bytes 4612
  0.0 39.3 %copy-start.2 = (f32[384]{0:T(512)S(1)}, f32[384]{0:T(512)}, u32[]{:S(2)}) copy-start(f32[384]{0:T(512)} %param.14) | copy-start | bytes 4612
  0.8 0.7 collective-permute-start
  7.3 28.8 %all-to-all-start = ((bf16[8,2,16,128]{3,2,1,0:T(8,128)(2,1)}), bf16[8,2,16,128]{3,2,1,0:T(8,128)(2,1)S(1)}, u32[]{:S(2)}, u32[]{:S(2)}) async-start(bf16[8,2,16,128]{3,2,1,0:T(8,128)(2,1)} %constant_dynamic-update-slice_fusion), calls=%async_computation | async-start | bytes 131072 | tf_op jit(solution)/shard_map/all_to_all | solution.py:268
  36.2 9.3 %collective-permute-start.1 = (bf16[12,16,128]{2,1,0:T(8,128)(2,1)S(1)}, bf16[12,16,128]{2,1,0:T(8,128)(2,1)S(1)}, u32[]{:S(2)}, u32[]{:S(2)}) collective-permute-start(bf16[12,16,128]{2,1,0:T(8,128)(2,1)S(1)} %pad_maximum_fusion.1), channel_id=1, source_target_pairs={{0,0},{1,8},{2,16},{3,24},{4,32},{5,40},{6,48},{7,56},{8,1},{9,9},... | collective-permute-start | bytes 147464 | tf_op jit(solution)/shard_map/ppermute | solution.py:271
where the time goes:
time: 112 us
  Pallas kernels  38.3 us (34%)
  starting transfers between devices  26.3 us (23%)
  blocking collectives  21 us (19%)
  local copies, waits for them, and re-layouts  14.8 us (13%)
  waiting for transfers between devices  9.56 us (9%)
  other arithmetic  1.52 us (1%)
    pallas_call x1, Pallas kernels, run_tile(): pl.pallas_call(functools.partial(tile_kernel, tr, tc, h, w, frames, (c_la...  38.3 us
    all_to_all x1, starting transfers between devices, gather_tile(): got = lax.all_to_all(blocks, 'rj', 0, 0, tiled=True)  23.7 us
    all_to_all x1, blocking collectives, per_device(): got = lax.all_to_all(send, 'rj', 0, 0, tiled=True)  21 us
    unnamed x18, local copies, waits for them, and re-layouts  6.3 us
    ppermute x1, waiting for transfers between devices, gather_tile(): pieces = lax.ppermute(pieces, ROW, swap)  4.98 us
    all_to_all x1, waiting for transfers between devices, gather_tile(): got = lax.all_to_all(blocks, 'rj', 0, 0, tiled=True)  4.59 us
  transfers between devices with their start and end apart: 3, of which 2 were waited for; matrix products, arithmetic and copies ran while one was open for 3% of the time, Pallas kernels for 0%

commit v1 on v0

--- a/solution.py
+++ b/solution.py
@@ -21,7 +21,7 @@
     c_lat, c_hi, c_mid, c_lo = dims
     (place, x, g1, g2, g3, g4, w_in, w_mid, w_up, w_low, w_out, out,
      win_v, wmid_v, wup_v, wlow_v, wout_v,
-     xf, x9, wt, first, act1, a9, second, act2, b9, wc, act3, c9, wl, a4, wo, zs, sems) = refs
+     xf, x9, wt, first, act1, im, second, act2, wc, act3, wl, a4, wo, zs, sems) = refs
     s = tc + 2 * HALO
     r_first, r_mid, r_up, r_low = tr + 6, tr + 4, tr + 2, tr + 1
     row0, col0 = place[0], place[1]
@@ -45,12 +45,15 @@
     def rms_act(v, gain, channels, mask):
         total = jnp.sum(v * v, axis=-1, keepdims=True)
         scale = lax.rsqrt(total * (1.0 / channels) + EPS) * mask
-        z = v * scale * gain
-        return 0.5 * z * (1.0 + jnp.tanh(0.5 * z))
+        z = v * scale * (0.5 * gain)
+        return z + z * jnp.tanh(z)
 
     k1 = 128
     xf[...] = jnp.zeros(xf.shape, F32)
-    xf[0 : x.shape[0], :] = x[...].astype(F32)
+    for k in range(x.shape[0]):
+        piece = x[k].astype(F32)
+        xf[pl.ds(2 * k, x.shape[1], stride=s), :] = piece
+        xf[pl.ds(2 * k + 1, x.shape[1], stride=s), :] = pltpu.roll(piece, 64, 1)
     m1 = r_first * s
     for b in range(3):
         for e in range(3):
@@ -70,13 +73,15 @@
         first[2 * half + 1] = y[:, c_hi:]
 
     def norm_one(i, carry):
-        t, r = i // r_first, i % r_first
-        v = first[t, pl.ds(pl.multiple_of(r * s, 8), s), :].reshape(1, s, c_hi)
-        y = rms_act(v, g1[...].reshape(1, 1, c_hi), c_hi, inside(1, r - 3, -3))
-        act1[t, pl.ds(pl.multiple_of(r * s, 8), s), :] = y.reshape(s, c_hi)
-        return carry
-
-    lax.fori_loop(0, frames * r_first, norm_one, 0, unroll=2)
+        steps = r_first // 2
+        t, r = i // steps, i % steps * 2
+        rows = pl.ds(pl.multiple_of(r * s, 8), 2 * s)
+        v = first[t, rows, :].reshape(2, s, c_hi)
+        y = rms_act(v, g1[...].reshape(1, 1, c_hi), c_hi, inside(2, r - 3, -3))
+        act1[t, rows, :] = y.reshape(2 * s, c_hi)
+        return carry
+
+    lax.fori_loop(0, frames * (r_first // 2), norm_one, 0, unroll=4)
     for t in range(frames):
         act1[t, m1:, :] = jnp.zeros((act1.shape[1] - m1, c_hi), F32)
 
@@ -86,7 +91,7 @@
         for b in range(3):
             for e in range(3):
                 tap = 3 * b + e
-                a9[t, :, tap * c_hi : (tap + 1) * c_hi] = act1[t, s * b + e : s * b + e + m2, :].astype(BF16)
+                im[pl.ds(pl.multiple_of(t * m2, 16), m2), tap * c_hi : (tap + 1) * c_hi] = act1[t, s * b + e : s * b + e + m2, :].astype(BF16)
         second[t] = first[t, s + 1 : s + 1 + m2, :]
         return carry
 
@@ -94,17 +99,21 @@
     for a in range(3):
         copies[1 + a].wait()
     for t in range(frames):
-        for d in range(min(3, frames - t)):
-            second[t + d] += jnp.dot(a9[t], wmid_v[:, d * c_hi : (d + 1) * c_hi], preferred_element_type=F32)
+        n = min(3, frames - t)
+        y = jnp.dot(im[t * m2 : (t + 1) * m2, :], wmid_v[:, : n * c_hi], preferred_element_type=F32)
+        for d in range(n):
+            second[t + d] += y[:, d * c_hi : (d + 1) * c_hi]
 
     def norm_two(i, carry):
-        t, r = i // r_mid, i % r_mid
-        v = second[t, pl.ds(pl.multiple_of(r * s, 8), s), :].reshape(1, s, c_hi)
-        y = rms_act(v, g2[...].reshape(1, 1, c_hi), c_hi, inside(1, r - 2, -2))
-        act2[t, pl.ds(pl.multiple_of(r * s, 8), s), :] = y.reshape(s, c_hi)
-        return carry
-
-    lax.fori_loop(0, frames * r_mid, norm_two, 0, unroll=2)
+        steps = r_mid // 2
+        t, r = i // steps, i % steps * 2
+        rows = pl.ds(pl.multiple_of(r * s, 8), 2 * s)
+        v = second[t, rows, :].reshape(2, s, c_hi)
+        y = rms_act(v, g2[...].reshape(1, 1, c_hi), c_hi, inside(2, r - 2, -2))
+        act2[t, rows, :] = y.reshape(2 * s, c_hi)
+        return carry
+
+    lax.fori_loop(0, frames * (r_mid // 2), norm_two, 0, unroll=4)
     for t in range(frames):
         act2[t, m2:, :] = jnp.zeros((act2.shape[1] - m2, c_hi), F32)
 
@@ -114,7 +123,7 @@
         for b in range(3):
             for e in range(3):
                 tap = 3 * b + e
-                b9[pl.ds(pl.multiple_of(t * m3, 16), m3), tap * c_hi : (tap + 1) * c_hi] = act2[t, s * b + e : s * b + e + m3, :].astype(BF16)
+                im[pl.ds(pl.multiple_of(t * m3, 16), m3), tap * c_hi : (tap + 1) * c_hi] = act2[t, s * b + e : s * b + e + m3, :].astype(BF16)
         return carry
 
     lax.fori_loop(0, frames, fill_up, 0)
@@ -143,8 +152,8 @@
             def up_pair(f, carry, p=p, q=q, mask=mask):
                 rows = pl.ds(pl.multiple_of(f * 2 * m3, 16), 2 * m3)
                 top, low = (3 * p + q) * c_hi, (3 * p + 3 + q) * c_hi
-                y = lax.dot_general(b9[rows, top : top + 2 * c_hi], wc[p, q, 0], NT, preferred_element_type=F32)
-                y = y + lax.dot_general(b9[rows, low : low + 2 * c_hi], wc[p, q, 1], NT, preferred_element_type=F32)
+                y = lax.dot_general(im[rows, top : top + 2 * c_hi], wc[p, q, 0], NT, preferred_element_type=F32)
+                y = y + lax.dot_general(im[rows, low : low + 2 * c_hi], wc[p, q, 1], NT, preferred_element_type=F32)
                 y = rms_act(y.reshape(2, r_up, s, c_mid), g3[...].reshape(1, 1, 1, c_mid), c_mid, mask[None])
                 y = y.reshape(2, m3, c_mid)
                 act3[2 * p + q, f, 0:m3, :] = jnp.concatenate([y[0], y[1]], axis=-1)
@@ -153,7 +162,7 @@
 
             lax.fori_loop(0, frames // 2, up_pair, 0)
 
-    m4 = c9.shape[1]
+    m4 = a4.shape[1]
     kt = 2 * c_mid
     copies[5].wait()
     wl[...] = jnp.zeros(wl.shape, BF16)
@@ -174,9 +183,9 @@
                         (pp, dr), (qq, dc) = where_from[p][b], where_from[q][e]
                         tap = 3 * b + e
                         at = s * dr + dc
-                        c9[f, :, tap * kt : (tap + 1) * kt] = act3[2 * pp + qq, f, at : at + m4, :].astype(BF16)
-            z0 = jnp.dot(c9[0], wl[...], preferred_element_type=F32)
-            z1 = jnp.dot(c9[1], wl[:, :256], preferred_element_type=F32) + z0[:, 256:]
+                        im[f * m4 : (f + 1) * m4, tap * kt : (tap + 1) * kt] = act3[2 * pp + qq, f, at : at + m4, :].astype(BF16)
+            z0 = jnp.dot(im[0:m4, :], wl[...], preferred_element_type=F32)
+            z1 = jnp.dot(im[m4 : 2 * m4, :], wl[:, :256], preferred_element_type=F32) + z0[:, 256:]
             mask = inside(r_low, -p, -q)
             for t in range(frames):
                 v = (z0 if t < 2 else z1)[: r_low * s, (t % 2) * 128 : (t % 2 + 1) * 128]
@@ -193,6 +202,8 @@
         zs[k, 0:m4, :] = lax.dot_general(a4[k], wo[...], NT, preferred_element_type=F32)
     m5 = tr * s
     where_from = (((1, 0), (0, 0), (1, 1)), ((0, 0), (1, 1), (0, 1)))
+    lane = lax.broadcasted_iota(jnp.int32, (1, 128), 1) & 31
+    packed = jnp.zeros((m5, 128), F32)
     for p in range(2):
         for q in range(2):
             total = jnp.zeros((m5, 128), F32)
@@ -200,17 +211,49 @@
                 for e in range(3):
                     (pp, dr), (qq, dc) = where_from[p][b], where_from[q][e]
                     part = zs[2 * pp + qq, s * dr + dc : s * dr + dc + m5, :]
-                    shift = 3 * (3 * b + e)
-                    total = total + (pltpu.roll(part, 128 - shift, 1) if shift else part)
-            out[2 * p + q] = total
+                    shift = (2 * q + p - (3 * b + e)) % 128
+                    total = total + (pltpu.roll(part, shift, 1) if shift else part)
+            k = 2 * q + p
+            packed = jnp.where((lane == k) | (lane == k + 9) | (lane == k + 18), total, packed)
+    for r in range(tr):
+        out[r] = packed[r * s : r * s + tc]
+
+
+def turn_kernel(frames, cols, x, out):
+    ch = x.shape[0] // (frames * cols)
+    v = x[...].astype(F32)
+    v = jnp.concatenate([v[(t * cols + c) * ch : (t * cols + c + 1) * ch] for c in range(cols) for t in range(frames)])
+    v = jnp.concatenate([v, jnp.zeros_like(v)], axis=1)
+    out[...] = v.T[: out.shape[0]].astype(BF16)
+
+
+def blocks_kernel(tr, mine, beside, out, tall):
+    h = mine.shape[0]
+    tall[...] = jnp.zeros(tall.shape, F32)
+    tall[0, HALO : HALO + h, :] = mine[...].astype(F32)
+    tall[1, HALO : HALO + h, :] = beside[...].astype(F32)
+    for i in range(out.shape[0]):
+        out[i] = tall[:, tr * i : tr * i + tr + 2 * HALO, :].astype(BF16)
+
+
+def rows_kernel(got, out, wide):
+    parts, tc, lanes = got.shape
+    v = got[...].reshape(parts * tc, lanes)
+    for q in range(2):
+        wide[pl.ds(q, parts * tc, stride=2), :] = pltpu.roll(v, lanes - 2 * q, 1) if q else v
+    turned = wide[...].T
+    for t in range(out.shape[0]):
+        for o in range(out.shape[1]):
+            out[t, o] = turned[32 * t + 9 * o : 32 * t + 9 * o + 2, :]
 
 
 def run_tile(place, x, g1, g2, g3, g4, w_in, w_mid, w_up, w_low, w_out, tr, tc, h, w, frames):
     c_lat, c_hi = w_in.shape[-2:]
     c_mid, c_lo = w_low.shape[-2:]
     s = tc + 2 * HALO
-    m1, m2, m3, m5 = (tr + 6) * s, (tr + 4) * s, (tr + 2) * s, tr * s
+    m1, m2, m3 = (tr + 6) * s, (tr + 4) * s, (tr + 2) * s
     m4 = -(-(tr + 1) * s // 16) * 16
+    im = frames * m2
     vmem = pl.BlockSpec(memory_space=pltpu.VMEM)
     anywhere = pl.BlockSpec(memory_space=pl.ANY)
     scratch = [
@@ -224,13 +267,11 @@
         pltpu.VMEM((9 * 128, frames * c_hi), BF16),
         pltpu.VMEM((frames, m1, c_hi), F32),
         pltpu.VMEM((frames, m1 + 8, c_hi), F32),
-        pltpu.VMEM((frames, m2, 9 * c_hi), BF16),
+        pltpu.VMEM((im, 9 * c_hi), BF16),
         pltpu.VMEM((frames, m2, c_hi), F32),
         pltpu.VMEM((frames, m2 + 8, c_hi), F32),
-        pltpu.VMEM((frames * m3, 9 * c_hi), BF16),
         pltpu.VMEM((2, 2, 2, c_mid, 2 * c_hi), BF16),
         pltpu.VMEM((4, frames // 2, m3 + 16, 2 * c_mid), F32),
-        pltpu.VMEM((2, m4, 18 * c_mid), BF16),
         pltpu.VMEM((18 * c_mid, 512), BF16),
         pltpu.VMEM((4, m4, frames * 128), BF16),
         pltpu.VMEM((128, frames * 128), BF16),
@@ -239,7 +280,7 @@
     ]
     return pl.pallas_call(
         functools.partial(tile_kernel, tr, tc, h, w, frames, (c_lat, c_hi, c_mid, c_lo)),
-        out_shape=jax.ShapeDtypeStruct((4, m5, 128), F32),
+        out_shape=jax.ShapeDtypeStruct((tr, tc, 128), F32),
         in_specs=[pl.BlockSpec(memory_space=pltpu.SMEM)] + [vmem] * 5 + [anywhere] * 5,
         out_specs=vmem,
         scratch_shapes=scratch,
@@ -248,10 +289,20 @@
     )(place, x, g1, g2, g3, g4, w_in, w_mid, w_up, w_low, w_out)
 
 
+def small_call(kernel, shape, dtype, scratch=(), name=None):
+    vmem = pl.BlockSpec(memory_space=pltpu.VMEM)
+    params = pltpu.CompilerParams(vmem_limit_bytes=4 * 1024 * 1024)
+    return pl.pallas_call(
+        kernel, out_shape=jax.ShapeDtypeStruct(shape, dtype), out_specs=vmem, scratch_shapes=list(scratch),
+        compiler_params=params, name=name,
+    )
+
+
 def gather_tile(latent, side, tr):
     frames, h, cols, ch = latent.shape
     lanes = frames * cols * ch
-    mine = jnp.transpose(latent, (1, 2, 0, 3)).reshape(h, lanes)
+    flat = jnp.transpose(latent, (0, 2, 3, 1)).reshape(lanes, h)
+    mine = small_call(functools.partial(turn_kernel, frames, cols), (h, lanes), BF16, name="turn")(flat)
     near = HALO // cols
     perm = []
     for g in range(side):
@@ -261,17 +312,13 @@
             if g > 0:
                 perm.append((g * side + k, (g - 1) * side + side - near + k))
     beside = lax.ppermute(mine, ROW, perm)
-    both = jnp.stack([mine, beside])
-    tall = jnp.pad(both, ((0, 0), (HALO, HALO), (0, 0)))
     rows = tr + 2 * HALO
-    blocks = jnp.stack([tall[:, tr * i : tr * i + rows] for i in range(side)])
+    tall = [pltpu.VMEM((2, h + 2 * HALO, lanes), F32)]
+    blocks = small_call(functools.partial(blocks_kernel, tr), (side, 2, rows, lanes), BF16, tall, "blocks")(mine, beside)
     got = lax.all_to_all(blocks, "rj", 0, 0, tiled=True)
     pieces = jnp.concatenate([got[:near, 1], got[:, 0], got[side - near :, 1]])
     swap = [(side * a + b, side * b + a) for a in range(side) for b in range(side)]
-    pieces = lax.ppermute(pieces, ROW, swap)
-    tile = pieces.reshape(-1, rows, cols, frames * ch).transpose(1, 0, 2, 3)
-    tile = tile.reshape(-1, frames * ch)
-    return jnp.pad(tile, ((0, 0), (0, 128 - frames * ch)))
+    return lax.ppermute(pieces, ROW, swap)
 
 
 def per_device(latent, w_in, gain_one, w_mid, gain_two, w_up, gain_three, w_low, gain_four, w_out):
@@ -279,22 +326,20 @@
     side = lax.axis_size("ri")
     w = cols * side * side
     tr, tc = h // side, w // side
-    s = tc + 2 * HALO
     x = gather_tile(latent, side, tr)
     place = jnp.stack([lax.axis_index("ri") * tr, lax.axis_index("rj") * tc]).astype(jnp.int32)
     c_lo, c_out = w_out.shape[-2:]
-    colour = jnp.transpose(w_out, (0, 1, 2, 4, 3)).reshape(3, 9 * c_out, c_lo)
+    colour = jnp.transpose(w_out, (0, 4, 1, 2, 3)).reshape(3, 9 * c_out, c_lo)
     colour = jnp.pad(colour, ((0, 0), (0, 32 - 9 * c_out), (0, 0)))
-    out = run_tile(
+    send = run_tile(
         place, x, gain_one[None], gain_two[None], gain_three[None],
         jnp.pad(gain_four, (0, 128 - c_lo))[None], w_in,
         w_mid.reshape(3, -1, w_mid.shape[-1]), jnp.transpose(w_up, (0, 1, 3, 2)), w_low, colour,
         tr, tc, h, w, frames,
     )
-    out = out.reshape(2, 2, tr, s, frames, 32)[:, :, :, :tc, :, :c_out]
-    send = jnp.transpose(out, (2, 4, 5, 0, 3, 1)).reshape(tr, frames * c_out * 2, 2 * tc)
     got = lax.all_to_all(send, "rj", 0, 0, tiled=True)
-    return jnp.transpose(got, (1, 0, 2)).reshape(frames, c_out, 2, 2 * w)
+    wide = [pltpu.VMEM((2 * w, 128), F32)]
+    return small_call(rows_kernel, (frames, c_out, 2, 2 * w), F32, wide, "rows")(got)
 
 
 def solution(mesh):

time: 112 us -> 98 us (0.88)
  local copies, waits for them, and re-layouts: 14.8 us -> 6.48 us
  Pallas kernels: 38.3 us -> 34.4 us
  waiting for transfers between devices: 9.56 us -> 6.83 us
  blocking collectives: 21 us -> 22.8 us
    pallas_call x1, Pallas kernels: 38.3 us -> 32.9 us  [run_tile(): pl.pallas_call(functools.partial(tile_kernel, tr, tc, h, w, frames, (c_la...]
    unnamed x18 -> x4, local copies, waits for them, and re-layouts: 6.3 us -> 1.37 us
    reshape x5 -> x1, local copies, waits for them, and re-layouts: 2.67 us -> 0.03 us  [per_device(): colour = jnp.transpose(w_out, (0, 4, 1, 2, 3)).reshape(3, 9 * c_out, c_lo)]
    ppermute x1, waiting for transfers between devices: 4.98 us -> 2.9 us  [gather_tile(): return lax.ppermute(pieces, ROW, swap)]
    all_to_all x1, blocking collectives: 21 us -> 22.8 us  [per_device(): got = lax.all_to_all(send, 'rj', 0, 0, tiled=True)]
    pallas_call x0 -> x3, Pallas kernels: none -> 1.5 us  [the longest x1 0.79 us: per_device(): small_call(rows_kernel, (frames, c_out, 2, 2 * w), F32, wide, 'rows')(got)]
    another operation x8 -> x0, local copies, waits for them, and re-layouts: 1.16 us -> none  [gather_tile(): blocks = jnp.stack([tall[:, tr * i:tr * i + rows] for i in range(side)])]
  transfers between devices with their start and end apart: 3 -> 3, of which waited for: 2 -> 2; matrix products, arithmetic and copies ran while one was open for 3% -> 6% of each run, Pallas kernels for 0% -> 0%
where the time goes in v1:
time: 98 us; the launch traced here: 97.5 us
  Pallas kernels  34.4 us (35%)
  starting transfers between devices  26.3 us (27%)
  blocking collectives  22.8 us (23%)
  waiting for transfers between devices  6.83 us (7%)
  local copies, waits for them, and re-layouts  6.48 us (7%)
    pallas_call x1, Pallas kernels, run_tile(): pl.pallas_call(functools.partial(tile_kernel, tr, tc, h, w, frames, (c_la...  32.9 us
    all_to_all x1, starting transfers between devices, gather_tile(): got = lax.all_to_all(blocks, 'rj', 0, 0, tiled=True)  23.7 us
    all_to_all x1, blocking collectives, per_device(): got = lax.all_to_all(send, 'rj', 0, 0, tiled=True)  22.8 us
    all_to_all x1, waiting for transfers between devices, gather_tile(): got = lax.all_to_all(blocks, 'rj', 0, 0, tiled=True)  3.93 us
    ppermute x1, waiting for transfers between devices, gather_tile(): return lax.ppermute(pieces, ROW, swap)  2.9 us
  transfers between devices with their start and end apart: 3, of which 2 were waited for; matrix products, arithmetic and copies ran while one was open for 6% of the time, Pallas kernels for 0%

profile of v1, /device:TPU:37, one launch (start us, length us, event | category | flops | bytes accessed | tf_op | source)
XLA Modules:
  0.0 97.5 jit_solution(14062363357671035468)
XLA Ops:
  0.0 0.0 copy-start
  0.0 0.8 copy-done
  0.8 0.1 turn.1.mine
  0.8 0.7 collective-permute-start
  1.5 0.0 collective-permute-done.beside
  1.5 0.6 blocks.1
  2.2 23.7 %all-to-all-start = ((bf16[8,2,16,128]{3,2,1,0:T(8,128)(2,1)}), bf16[8,2,16,128]{3,2,1,0:T(8,128)(2,1)S(1)}, u32[]{:S(2)}, u32[]{:S(2)}) async-start(bf16[8,2,16,128]{3,2,1,0:T(8,128)(2,1)} %blocks.1), calls=%async_computation | async-start | bytes 131072 | tf_op jit(solution)/shard_map/all_to_all | solution.py:318
  25.8 1.2 %pad_bitcast_fusion.refs_5_ = f32[1,128]{1,0:T(1,128)} fusion(f32[96]{0:T(128)} %param.18), kind=kLoop, calls=%fused_computation.5 | loop fusion | bytes 896 | tf_op jit(solution)/shard_map/broadcast_in_dim | solution.py:336
  27.1 3.9 %all-to-all-done = bf16[8,2,16,128]{3,2,1,0:T(8,128)(2,1)S(1)} async-done(((bf16[8,2,16,128]{3,2,1,0:T(8,128)(2,1)}), bf16[8,2,16,128]{3,2,1,0:T(8,128)(2,1)S(1)}, u32[]{:S(2)}, u32[]{:S(2)}) %all-to-all-start) | async-done | bytes 65568 | tf_op jit(solution)/shard_map/all_to_all | solution.py:318
  31.0 2.0 %collective-permute-start.1 = (bf16[12,16,128]{2,1,0:T(8,128)(2,1)S(1)}, bf16[12,16,128]{2,1,0:T(8,128)(2,1)S(1)}, u32[]{:S(2)}, u32[]{:S(2)}) collective-permute-start(bf16[12,16,128]{2,1,0:T(8,128)(2,1)S(1)} %pad_maximum_fusion), channel_id=1, source_target_pairs={{0,0},{1,8},{2,16},{3,24},{4,32},{5,40},{6,48},{7,56},{8,1},{9,9},... | collective-permute-start | bytes 147464 | tf_op jit(solution)/shard_map/ppermute | solution.py:321
  33.0 0.6 pad_add_fusion.refs_0_
  33.6 0.8 copy.16
  34.4 1.2 %broadcast_in_dim.12.refs_2_ = f32[1,384]{1,0:T(1,128)} reshape(f32[384]{0:T(512)} %param.12) | data formatting | bytes 3072 | tf_op jit(solution)/shard_map/broadcast_in_dim | solution.py:335
  35.6 1.2 %broadcast_in_dim.13.refs_3_ = f32[1,384]{1,0:T(1,128)} reshape(f32[384]{0:T(512)} %param.14) | data formatting | bytes 3072 | tf_op jit(solution)/shard_map/broadcast_in_dim | solution.py:335
  36.8 0.6 pad.9.refs_10_
  37.5 2.9 %collective-permute-done.1.refs_1_ = bf16[12,16,128]{2,1,0:T(8,128)(2,1)S(1)} collective-permute-done((bf16[12,16,128]{2,1,0:T(8,128)(2,1)S(1)}, bf16[12,16,128]{2,1,0:T(8,128)(2,1)S(1)}, u32[]{:S(2)}, u32[]{:S(2)}) %collective-permute-start.1) | collective-permute-done | bytes 49184 | tf_op jit(solution)/shard_map/ppermute | solution.py:321
  40.4 0.0 copy-start.1
  40.4 0.6 copy-done.1
  41.0 32.9 %tile.1 = f32[8,16,128]{2,1,0:T(8,128)} custom-call(s32[2]{0:T(128)} %pad_add_fusion.refs_0_, bf16[12,16,128]{2,1,0:T(8,128)(2,1)} %copy-done.1, f32[1,384]{1,0:T(1,128)} %broadcast_in_dim.12.refs_2_, f32[1,384]{1,0:T(1,128)} %broadcast_in_dim.13.refs_3_, f32[1,192]{1,0:T(1,128)} %bitcast.27, f32[1,128]{1,0:T(1,128)} %pad_bitcast_fusion.refs_5_, ...), custom_call_target="tpu_custom_call" | custom-call | tf_op jit(solution)/shard_map/tile/pallas_call | solution.py:281
  73.9 22.8 %all_to_all.10.got = f32[8,16,128]{2,1,0:T(8,128)S(1)} all-to-all(f32[8,16,128]{2,1,0:T(8,128)} %tile.1), channel_id=1, replica_groups=mesh['groups'=4,'ri'=8,'rj'=8] {'rj'}, dimensions={0} | all-to-all | bytes 131072 | tf_op jit(solution)/shard_map/all_to_all | solution.py:340
  96.7 0.8 rows.1
  (4 shorter events, 0.0 us)
Async XLA Ops:
  0.0 0.8 copy-start
  0.8 0.7 collective-permute-start
  2.2 28.8 %all-to-all-start = ((bf16[8,2,16,128]{3,2,1,0:T(8,128)(2,1)}), bf16[8,2,16,128]{3,2,1,0:T(8,128)(2,1)S(1)}, u32[]{:S(2)}, u32[]{:S(2)}) async-start(bf16[8,2,16,128]{3,2,1,0:T(8,128)(2,1)} %blocks.1), calls=%async_computation | async-start | bytes 131072 | tf_op jit(solution)/shard_map/all_to_all | solution.py:318
  31.0 9.3 %collective-permute-start.1 = (bf16[12,16,128]{2,1,0:T(8,128)(2,1)S(1)}, bf16[12,16,128]{2,1,0:T(8,128)(2,1)S(1)}, u32[]{:S(2)}, u32[]{:S(2)}) collective-permute-start(bf16[12,16,128]{2,1,0:T(8,128)(2,1)S(1)} %pad_maximum_fusion), channel_id=1, source_target_pairs={{0,0},{1,8},{2,16},{3,24},{4,32},{5,40},{6,48},{7,56},{8,1},{9,9},... | collective-permute-start | bytes 147464 | tf_op jit(solution)/shard_map/ppermute | solution.py:321
  40.4 0.6 copy-start.1

commit v2 on v1

v2 whole, which is shorter than its diff:
```python
import functools
import math

import jax
import jax.numpy as jnp
from jax import lax
from jax.experimental import pallas as pl
from jax.experimental.pallas import tpu as pltpu
from jax.sharding import Mesh
from jax.sharding import PartitionSpec as P

ROW = ("ri", "rj")
EPS = 1e-06
TILE_MIB = 36
WEIGHTS_MIB = 8
HALO = 4
F32 = jnp.float32
BF16 = jnp.bfloat16
NT = (((1,), (1,)), ((), ()))


def weights_kernel(frames, dims, *refs):
    c_lat, c_hi, c_mid, c_lo = dims
    (after, w_in, w_mid, w_up, w_low, w_out, wt, wmid, wc, wl, wo, win_v, wup_v, wlow_v, wout_v, sems) = refs
    copies = [
        pltpu.make_async_copy(w_in, win_v, sems.at[0]),
        pltpu.make_async_copy(w_up, wup_v, sems.at[1]),
        pltpu.make_async_copy(w_low, wlow_v, sems.at[2]),
        pltpu.make_async_copy(w_out, wout_v, sems.at[3]),
    ]
    for a in range(3):
        dst = wmid.at[:, (2 - a) * c_hi : (3 - a) * c_hi]
        copies.append(pltpu.make_async_copy(w_mid.at[a], dst, sems.at[4 + a]))
    for copy in copies:
        copy.start()

    k1 = 128
    wt[...] = jnp.zeros(wt.shape, BF16)
    wl[...] = jnp.zeros(wl.shape, BF16)
    wo[...] = jnp.zeros(wo.shape, BF16)
    copies[0].wait()
    for b in range(3):
        for e in range(3):
            for ti in range(frames):
                for to in range(ti, min(frames, ti + 3)):
                    at = (3 * b + e) * k1 + ti * c_lat
                    wt[at : at + c_lat, to * c_hi : (to + 1) * c_hi] = win_v[ti - to + 2, b, e]

    copies[1].wait()

    def pairs(k):
        return (k[0], k[1] + k[2]), (k[0] + k[1], k[2])

    def combine(i, carry):
        at = pl.ds(pl.multiple_of(i * 32, 32), 32)
        tap = [[wup_v[b, e, at, :].astype(F32) for e in range(3)] for b in range(3)]
        by_row = [pairs([tap[b][e] for b in range(3)]) for e in range(3)]
        for p in range(2):
            for bb in range(2):
                by_col = pairs([by_row[e][p][bb] for e in range(3)])
                for q in range(2):
                    for ee in range(2):
                        wc[p, q, bb, at, ee * c_hi : (ee + 1) * c_hi] = by_col[q][ee].astype(BF16)
        return carry

    lax.fori_loop(0, c_mid // 32, combine, 0)

    kt = 2 * c_mid
    copies[2].wait()
    for b in range(3):
        for e in range(3):
            at = (3 * b + e) * kt
            for fi in range(2):
                for to in range(4):
                    a = fi - to + 2
                    if 0 <= a <= 2:
                        wl[at + fi * c_mid : at + (fi + 1) * c_mid, to * 128 : to * 128 + c_lo] = wlow_v[a, b, e]
    copies[3].wait()
    for ti in range(frames):
        for to in range(ti, min(frames, ti + 3)):
            wo[to * 32 : (to + 1) * 32, ti * 128 : ti * 128 + c_lo] = wout_v[ti - to + 2]
    for copy in copies[4:]:
        copy.wait()


def tile_kernel(tr, tc, h, w, frames, dims, *refs):
    c_lat, c_hi, c_mid, c_lo = dims
    (place, x, g1, g2, g3, g4, wt, wmid, wc, wl, wo, out,
     xf, x9, first, act1, im, second, act2, third, act3, fourth, a4, zs) = refs
    s = tc + 2 * HALO
    r_first, r_mid, r_up, r_low = tr + 6, tr + 4, tr + 2, tr + 1
    row0, col0 = place[0], place[1]

    def inside(rows, row_shift, col_shift):
        r = lax.broadcasted_iota(jnp.int32, (rows, s, 1), 0) + (row0 + row_shift)
        c = lax.broadcasted_iota(jnp.int32, (rows, s, 1), 1) + (col0 + col_shift)
        ok = (r >= 0) & (r < h) & (c >= 0) & (c < w)
        return jnp.where(ok, 1.0, 0.0).astype(F32)

    def rms_act(v, gain, channels, mask):
        total = jnp.sum(v * v, axis=-1, keepdims=True)
        scale = lax.rsqrt(total * (1.0 / channels) + EPS) * mask
        z = v * scale * (0.5 * gain)
        return z + z * jnp.tanh(z)

    k1 = 128
    xf[...] = jnp.zeros(xf.shape, F32)
    for k in range(x.shape[0]):
        piece = x[k].astype(F32)
        xf[pl.ds(2 * k, x.shape[1], stride=s), :] = piece
        xf[pl.ds(2 * k + 1, x.shape[1], stride=s), :] = pltpu.roll(piece, 64, 1)
    m1 = r_first * s
    for b in range(3):
        for e in range(3):
            tap = 3 * b + e
            x9[:, tap * k1 : (tap + 1) * k1] = xf[s * b + e : s * b + e + m1, :].astype(BF16)
    for half in range(frames // 2):
        y = jnp.dot(x9[...], wt[:, half * 2 * c_hi : (half + 1) * 2 * c_hi], preferred_element_type=F32)
        first[2 * half] = y[:, :c_hi]
        first[2 * half + 1] = y[:, c_hi:]

    def norm_one(i, carry):
        steps = r_first // 2
        t, r = i // steps, i % steps * 2
        rows = pl.ds(pl.multiple_of(r * s, 8), 2 * s)
        v = first[t, rows, :].reshape(2, s, c_hi)
        y = rms_act(v, g1[...].reshape(1, 1, c_hi), c_hi, inside(2, r - 3, -3))
        act1[t, rows, :] = y.reshape(2 * s, c_hi)
        return carry

    lax.fori_loop(0, frames * (r_first // 2), norm_one, 0, unroll=4)
    for t in range(frames):
        act1[t, m1:, :] = jnp.zeros((act1.shape[1] - m1, c_hi), F32)

    m2 = r_mid * s
    for t in range(frames):
        second[t] = first[t, s + 1 : s + 1 + m2, :]
    for t in range(frames):
        for b in range(3):
            for e in range(3):
                tap = 3 * b + e
                im[t * m2 : (t + 1) * m2, tap * c_hi : (tap + 1) * c_hi] = act1[t, s * b + e : s * b + e + m2, :].astype(BF16)
        n = min(3, frames - t)
        y = jnp.dot(im[t * m2 : (t + 1) * m2, :], wmid[:, : n * c_hi], preferred_element_type=F32)
        for d in range(n):
            second[t + d] += y[:, d * c_hi : (d + 1) * c_hi]

    def norm_two(i, carry):
        steps = r_mid // 2
        t, r = i // steps, i % steps * 2
        rows = pl.ds(pl.multiple_of(r * s, 8), 2 * s)
        v = second[t, rows, :].reshape(2, s, c_hi)
        y = rms_act(v, g2[...].reshape(1, 1, c_hi), c_hi, inside(2, r - 2, -2))
        act2[t, rows, :] = y.reshape(2 * s, c_hi)
        return carry

    lax.fori_loop(0, frames * (r_mid // 2), norm_two, 0, unroll=4)
    for t in range(frames):
        act2[t, m2:, :] = jnp.zeros((act2.shape[1] - m2, c_hi), F32)

    m3 = r_up * s
    for t in range(frames):
        for b in range(3):
            for e in range(3):
                tap = 3 * b + e
                im[t * m3 : (t + 1) * m3, tap * c_hi : (tap + 1) * c_hi] = act2[t, s * b + e : s * b + e + m3, :].astype(BF16)
        rows = slice(t * m3, (t + 1) * m3)
        for p in range(2):
            for q in range(2):
                top, low = (3 * p + q) * c_hi, (3 * p + 3 + q) * c_hi
                y = lax.dot_general(im[rows, top : top + 2 * c_hi], wc[p, q, 0], NT, preferred_element_type=F32)
                y = y + lax.dot_general(im[rows, low : low + 2 * c_hi], wc[p, q, 1], NT, preferred_element_type=F32)
                third[2 * p + q, t] = y

    def norm_three(i, carry):
        steps = r_up // 2
        k, r = i // steps, i % steps * 2
        rows = pl.ds(pl.multiple_of(r * s, 8), 2 * s)
        mask = inside(2, r - 1, -1)
        for f in range(frames // 2):
            ys = []
            for t in (2 * f, 2 * f + 1):
                v = third[k, t, rows, :].reshape(2, s, c_mid)
                ys.append(rms_act(v, g3[...].reshape(1, 1, c_mid), c_mid, mask).reshape(2 * s, c_mid))
            act3[k, f, rows, :] = jnp.concatenate(ys, axis=-1)
        return carry

    lax.fori_loop(0, 4 * (r_up // 2), norm_three, 0, unroll=2)
    for k in range(4):
        for f in range(frames // 2):
            act3[k, f, m3:, :] = jnp.zeros((act3.shape[2] - m3, 2 * c_mid), F32)

    last_gain = jnp.concatenate([g4[...].reshape(1, c_lo), jnp.zeros((1, 128 - c_lo), F32)], axis=1).reshape(1, 1, 128)
    m4 = a4.shape[1]
    kt = 2 * c_mid
    where_from = (((1, 0), (0, 1), (1, 1)), ((0, 0), (1, 0), (0, 1)))
    for p in range(2):
        for q in range(2):
            k = 2 * p + q
            base = (k % 2) * 2 * m4
            for f in range(2):
                for b in range(3):
                    for e in range(3):
                        (pp, dr), (qq, dc) = where_from[p][b], where_from[q][e]
                        tap = 3 * b + e
                        at = s * dr + dc
                        im[base + f * m4 : base + (f + 1) * m4, tap * kt : (tap + 1) * kt] = act3[2 * pp + qq, f, at : at + m4, :].astype(BF16)
            z0 = jnp.dot(im[base : base + m4, :], wl[...], preferred_element_type=F32)
            z1 = jnp.dot(im[base + m4 : base + 2 * m4, :], wl[:, :256], preferred_element_type=F32)
            z1 = z1 + z0[:, 256:]
            mask = inside(r_low, -p, -q)
            for t in range(frames):
                v = (z0 if t < 2 else z1)[: r_low * s, (t % 2) * 128 : (t % 2 + 1) * 128]
                y = rms_act(v.reshape(r_low, s, 128), last_gain, c_lo, mask)
                a4[k, 0 : r_low * s, t * 128 : (t + 1) * 128] = y.reshape(r_low * s, 128).astype(BF16)
            a4[k, r_low * s :, :] = jnp.zeros((m4 - r_low * s, frames * 128), BF16)

    for k in range(4):
        zs[k, 0:m4, :] = lax.dot_general(a4[k], wo[...], NT, preferred_element_type=F32)
    m5 = tr * s
    where_from = (((1, 0), (0, 0), (1, 1)), ((0, 0), (1, 1), (0, 1)))
    lane = lax.broadcasted_iota(jnp.int32, (1, 128), 1) & 31
    packed = jnp.zeros((m5, 128), F32)
    for p in range(2):
        for q in range(2):
            total = jnp.zeros((m5, 128), F32)
            for b in range(3):
                for e in range(3):
                    (pp, dr), (qq, dc) = where_from[p][b], where_from[q][e]
                    part = zs[2 * pp + qq, s * dr + dc : s * dr + dc + m5, :]
                    shift = (2 * q + p - (3 * b + e)) % 128
                    total = total + (pltpu.roll(part, shift, 1) if shift else part)
            k = 2 * q + p
            packed = jnp.where((lane == k) | (lane == k + 9) | (lane == k + 18), total, packed)
    for r in range(tr):
        out[r] = packed[r * s : r * s + tc]


def turn_kernel(frames, cols, x, out):
    ch = x.shape[0] // (frames * cols)
    v = x[...].astype(F32)
    v = jnp.concatenate([v[(t * cols + c) * ch : (t * cols + c + 1) * ch] for c in range(cols) for t in range(frames)])
    v = jnp.concatenate([v, jnp.zeros_like(v)], axis=1)
    out[...] = v.T[: out.shape[0]].astype(BF16)


def blocks_kernel(tr, mine, beside, out, tall):
    h = mine.shape[0]
    tall[...] = jnp.zeros(tall.shape, F32)
    tall[0, HALO : HALO + h, :] = mine[...].astype(F32)
    tall[1, HALO : HALO + h, :] = beside[...].astype(F32)
    for i in range(out.shape[0]):
        out[i] = tall[:, tr * i : tr * i + tr + 2 * HALO, :].astype(BF16)


def rows_kernel(got, out, wide):
    parts, tc, lanes = got.shape
    v = got[...].reshape(parts * tc, lanes)
    for q in range(2):
        wide[pl.ds(q, parts * tc, stride=2), :] = pltpu.roll(v, lanes - 2 * q, 1) if q else v
    turned = wide[...].T
    for t in range(out.shape[0]):
        for o in range(out.shape[1]):
            out[t, o] = turned[32 * t + 9 * o : 32 * t + 9 * o + 2, :]


def make_weights(after, w_in, w_mid, w_up, w_low, w_out, frames):
    c_lat, c_hi = w_in.shape[-2:]
    c_mid, c_lo = w_low.shape[-2:]
    vmem = pl.BlockSpec(memory_space=pltpu.VMEM)
    anywhere = pl.BlockSpec(memory_space=pl.ANY)
    shapes = (
        (9 * 128, frames * c_hi), (9 * c_hi, 3 * c_hi), (2, 2, 2, c_mid, 2 * c_hi), (18 * c_mid, 512), (128, frames * 128),
    )
    return pl.pallas_call(
        functools.partial(weights_kernel, frames, (c_lat, c_hi, c_mid, c_lo)),
        out_shape=[jax.ShapeDtypeStruct(shape, BF16) for shape in shapes],
        in_specs=[anywhere] * 6,
        out_specs=[vmem] * 5,
        scratch_shapes=[pltpu.VMEM(v.shape, BF16) for v in (w_in, w_up, w_low, w_out)] + [pltpu.SemaphoreType.DMA((7,))],
        compiler_params=pltpu.CompilerParams(vmem_limit_bytes=WEIGHTS_MIB * 1024 * 1024),
        name="weights",
    )(after, w_in, w_mid, w_up, w_low, w_out)


def run_tile(place, x, g1, g2, g3, g4, weights, dims, tr, tc, h, w, frames):
    c_lat, c_hi, c_mid, c_lo = dims
    s = tc + 2 * HALO
    m1, m2, m3 = (tr + 6) * s, (tr + 4) * s, (tr + 2) * s
    m4 = -(-(tr + 1) * s // 16) * 16
    vmem = pl.BlockSpec(memory_space=pltpu.VMEM)
    scratch = [
        pltpu.VMEM((m1 + 2 * s + 8, 128), F32),
        pltpu.VMEM((m1, 9 * 128), BF16),
        pltpu.VMEM((frames, m1, c_hi), F32),
        pltpu.VMEM((frames, m1 + 8, c_hi), F32),
        pltpu.VMEM((frames * m2, 9 * c_hi), BF16),
        pltpu.VMEM((frames, m2, c_hi), F32),
        pltpu.VMEM((frames, m2 + 8, c_hi), F32),
        pltpu.VMEM((4, frames, m3, c_mid), F32),
        pltpu.VMEM((4, frames // 2, m3 + 16, 2 * c_mid), F32),
        pltpu.VMEM((4, m4, frames * 128), F32),
        pltpu.VMEM((4, m4, frames * 128), BF16),
        pltpu.VMEM((4, m4 + 8, 128), F32),
    ]
    return pl.pallas_call(
        functools.partial(tile_kernel, tr, tc, h, w, frames, dims),
        out_shape=jax.ShapeDtypeStruct((tr, tc, 128), F32),
        in_specs=[pl.BlockSpec(memory_space=pltpu.SMEM)] + [vmem] * 10,
        out_specs=vmem,
        scratch_shapes=scratch,
        compiler_params=pltpu.CompilerParams(vmem_limit_bytes=TILE_MIB * 1024 * 1024),
        name="tile",
    )(place, x, g1, g2, g3, g4, *weights)


def small_call(kernel, shape, dtype, scratch=(), name=None):
    vmem = pl.BlockSpec(memory_space=pltpu.VMEM)
    params = pltpu.CompilerParams(vmem_limit_bytes=4 * 1024 * 1024)
    return pl.pallas_call(
        kernel, out_shape=jax.ShapeDtypeStruct(shape, dtype), out_specs=vmem, scratch_shapes=list(scratch),
        compiler_params=params, name=name,
    )


def gather_tile(latent, side, tr):
    frames, h, cols, ch = latent.shape
    lanes = frames * cols * ch
    flat = jnp.transpose(latent, (0, 2, 3, 1)).reshape(lanes, h)
    mine = small_call(functools.partial(turn_kernel, frames, cols), (h, lanes), BF16, name="turn")(flat)
    near = HALO // cols
    perm = []
    for g in range(side):
        for k in range(near):
            if g + 1 < side:
                perm.append((g * side + side - near + k, (g + 1) * side + k))
            if g > 0:
                perm.append((g * side + k, (g - 1) * side + side - near + k))
    beside = lax.ppermute(mine, ROW, perm)
    rows = tr + 2 * HALO
    tall = [pltpu.VMEM((2, h + 2 * HALO, lanes), F32)]
    blocks = small_call(functools.partial(blocks_kernel, tr), (side, 2, rows, lanes), BF16, tall, "blocks")(mine, beside)
    got = lax.all_to_all(blocks, "rj", 0, 0, tiled=True)
    pieces = jnp.concatenate([got[:near, 1], got[:, 0], got[side - near :, 1]])
    swap = [(side * a + b, side * b + a) for a in range(side) for b in range(side)]
    return lax.ppermute(pieces, ROW, swap), pieces


def per_device(latent, w_in, gain_one, w_mid, gain_two, w_up, gain_three, w_low, gain_four, w_out):
    frames, h, cols, _ = latent.shape
    side = lax.axis_size("ri")
    w = cols * side * side
    tr, tc = h // side, w // side
    x = gather_tile(latent, side, tr)
    place = jnp.stack([lax.axis_index("ri") * tr, lax.axis_index("rj") * tc]).astype(jnp.int32)
    c_lo, c_out = w_out.shape[-2:]
    colour = jnp.transpose(w_out, (0, 4, 1, 2, 3)).reshape(3, 9 * c_out, c_lo)
    colour = jnp.pad(colour, ((0, 0), (0, 32 - 9 * c_out), (0, 0)))
    weights = make_weights(
        x[1], w_in, w_mid.reshape(3, -1, w_mid.shape[-1]), jnp.transpose(w_up, (0, 1, 3, 2)), w_low, colour, frames
    )
    dims = w_in.shape[-2:] + w_low.shape[-2:]
    send = run_tile(
        place, x[0], gain_one, gain_two, gain_three, gain_four, weights, dims, tr, tc, h, w, frames,
    )
    got = lax.all_to_all(send, "rj", 0, 0, tiled=True)
    wide = [pltpu.VMEM((2 * w, 128), F32)]
    return small_call(rows_kernel, (frames, c_out, 2, 2 * w), F32, wide, "rows")(got)


def solution(mesh):
    side = math.isqrt(mesh.shape["row"])
    grid = Mesh(mesh.devices.reshape(mesh.shape["groups"], side, side), ("groups",) + ROW)
    in_specs = (P("groups", None, ROW, None),) + (P(),) * 9
    out_specs = P("groups", None, ROW, None)
    return jax.shard_map(per_device, mesh=grid, in_specs=in_specs, out_specs=out_specs, check_vma=False)
```

time: 98 us -> 98.2 us (level)
  blocking collectives: 22.8 us -> 25.5 us
  Pallas kernels: 34.4 us -> 32.1 us
  local copies, waits for them, and re-layouts: 6.48 us -> 8.45 us
  waiting for transfers between devices: 6.83 us -> 5.16 us
    unnamed x4 -> x18, local copies, waits for them, and re-layouts: 1.37 us -> 7.64 us
    broadcast_in_dim x3 -> x0, local copies, waits for them, and re-layouts: 3.7 us -> none  [the longest x1 1.25 us: per_device(): gain_one[None]]
    ppermute x1, waiting for transfers between devices: 2.9 us -> 0.01 us  [gather_tile(): return (lax.ppermute(pieces, ROW, swap), pieces)]
    all_to_all x1, blocking collectives: 22.8 us -> 25.5 us  [per_device(): got = lax.all_to_all(send, 'rj', 0, 0, tiled=True)]
    pallas_call x1 -> x2, Pallas kernels: 32.9 us -> 30.6 us  [the longest x1 28 us: run_tile(): pl.pallas_call(functools.partial(tile_kernel, tr, tc, h, w, frames, dims)...]
    all_to_all x1, waiting for transfers between devices: 3.93 us -> 5.16 us  [gather_tile(): got = lax.all_to_all(blocks, 'rj', 0, 0, tiled=True)]
  transfers between devices with their start and end apart: 3 -> 3, of which waited for: 2 -> 1; matrix products, arithmetic and copies ran while one was open for 6% -> 1% of each run, Pallas kernels for 0% -> 3%
where the time goes in v2:
time: 98.2 us; the launch traced here: 97.7 us
  Pallas kernels  32.1 us (33%)
  starting transfers between devices  26.3 us (27%)
  blocking collectives  25.5 us (26%)
  local copies, waits for them, and re-layouts  8.45 us (9%)
  waiting for transfers between devices  5.16 us (5%)
    pallas_call x1, Pallas kernels, run_tile(): pl.pallas_call(functools.partial(tile_kernel, tr, tc, h, w, frames, dims)...  28 us
    all_to_all x1, blocking collectives, per_device(): got = lax.all_to_all(send, 'rj', 0, 0, tiled=True)  25.5 us
    all_to_all x1, starting transfers between devices, gather_tile(): got = lax.all_to_all(blocks, 'rj', 0, 0, tiled=True)  23.7 us
    unnamed x18, local copies, waits for them, and re-layouts  7.64 us
    all_to_all x1, waiting for transfers between devices, gather_tile(): got = lax.all_to_all(blocks, 'rj', 0, 0, tiled=True)  5.16 us
    pallas_call x1, Pallas kernels, make_weights(): pl.pallas_call(functools.partial(weights_kernel, frames, (c_lat, c_hi, c_...  2.58 us
  transfers between devices with their start and end apart: 3, of which 1 were waited for; matrix products, arithmetic and copies ran while one was open for 1% of the time, Pallas kernels for 3%

profile of v2, /device:TPU:37, one launch (start us, length us, event | category | flops | bytes accessed | tf_op | source)
XLA Modules:
  0.0 97.7 jit_solution(3824041520364778483)
XLA Ops:
  0.0 0.0 copy-start.4
  0.0 0.8 copy-done.4
  0.8 0.1 turn.1.mine
  0.8 0.7 collective-permute-start
  1.5 0.0 collective-permute-done.beside
  1.5 0.6 blocks.1
  2.2 23.7 %all-to-all-start = ((bf16[8,2,16,128]{3,2,1,0:T(8,128)(2,1)}), bf16[8,2,16,128]{3,2,1,0:T(8,128)(2,1)S(1)}, u32[]{:S(2)}, u32[]{:S(2)}) async-start(bf16[8,2,16,128]{3,2,1,0:T(8,128)(2,1)} %blocks.1), calls=%async_computation | async-start | bytes 131072 | tf_op jit(solution)/shard_map/all_to_all | solution.py:343
  25.8 5.2 %all-to-all-done = bf16[8,2,16,128]{3,2,1,0:T(8,128)(2,1)S(1)} async-done(((bf16[8,2,16,128]{3,2,1,0:T(8,128)(2,1)}), bf16[8,2,16,128]{3,2,1,0:T(8,128)(2,1)S(1)}, u32[]{:S(2)}, u32[]{:S(2)}) %all-to-all-start) | async-done | bytes 65568 | tf_op jit(solution)/shard_map/all_to_all | solution.py:343
  31.0 2.0 %collective-permute-start.1 = (bf16[12,16,128]{2,1,0:T(8,128)(2,1)S(1)}, bf16[12,16,128]{2,1,0:T(8,128)(2,1)S(1)}, u32[]{:S(2)}, u32[]{:S(2)}) collective-permute-start(bf16[12,16,128]{2,1,0:T(8,128)(2,1)S(1)} %pad_maximum_fusion.refs_0_), channel_id=1, source_target_pairs={{0,0},{1,8},{2,16},{3,24},{4,32},{5,40},{6,48},{7,56},{8,1},{9,9},... | collective-permute-start | bytes 147464 | tf_op jit(solution)/shard_map/ppermute | solution.py:346
  33.0 0.1 pad_add_fusion.refs_0_
  33.0 0.8 copy.16
  33.9 0.0 copy-start
  33.9 3.3 %copy-done = bf16[3,3,3,384,384]{4,3,2,1,0:T(8,128)(2,1)S(1)} copy-done((bf16[3,3,3,384,384]{4,3,2,1,0:T(8,128)(2,1)S(1)}, bf16[3,3,3,384,384]{4,3,2,1,0:T(8,128)(2,1)}, u32[]{:S(2)}) %copy-start) | copy-done | bytes 7962648
  37.1 0.0 copy-start.1
  37.1 1.3 %copy-done.1 = bf16[3,3,384,192]{2,3,1,0:T(8,128)(2,1)S(1)} copy-done((bf16[3,3,384,192]{2,3,1,0:T(8,128)(2,1)S(1)}, bf16[3,3,384,192]{2,3,1,0:T(8,128)(2,1)}, u32[]{:S(2)}) %copy-start.1) | copy-done | bytes 1327128
  38.4 0.0 copy-start.2
  38.4 1.3 %copy-done.2 = bf16[3,3,3,192,96]{4,3,2,1,0:T(8,128)(2,1)S(1)} copy-done((bf16[3,3,3,192,96]{4,3,2,1,0:T(8,128)(2,1)S(1)}, bf16[3,3,3,192,96]{4,3,2,1,0:T(8,128)(2,1)}, u32[]{:S(2)}) %copy-start.2) | copy-done | bytes 995352
  39.8 0.0 copy-start.3
  39.8 1.0 copy-done.3
  40.7 0.0 copy-start.5
  40.7 0.0 copy-start.6
  40.7 0.0 copy-start.7
  40.7 0.0 copy-start.8
  40.7 2.6 %weights.1 = (bf16[1152,1536]{1,0:T(8,128)(2,1)S(1)}, bf16[3456,1152]{1,0:T(8,128)(2,1)S(1)}, bf16[2,2,2,192,768]{4,3,2,1,0:T(8,128)(2,1)S(1)}, bf16[3456,512]{1,0:T(8,128)(2,1)S(1)}, bf16[128,512]{1,0:T(8,128)(2,1)S(1)}) custom-call(bf16[12,16,128]{2,1,0:T(8,128)(2,1)S(1)} %pad_maximum_fusion.refs_0_, bf16[3,3,3,16,384]{4,3,2,1,0:T(8,128)(2,1)S(1)} %copy-done.3, ...), custom_call_target="tpu_custom_call" | custom-call | tf_op jit(solution)/shard_map/weights/pallas_call | solution.py:275
  43.3 0.0 collective-permute-done.1.refs_1_
  43.3 0.0 copy-done.5
  43.3 0.0 copy-done.6
  43.4 0.0 copy-done.7
  43.4 0.0 copy-done.8
  43.4 28.0 %tile.1 = f32[8,16,128]{2,1,0:T(8,128)S(1)} custom-call(s32[2]{0:T(128)S(1)} %pad_add_fusion.refs_0_, bf16[12,16,128]{2,1,0:T(8,128)(2,1)S(1)} %collective-permute-done.1.refs_1_, f32[384]{0:T(512)S(1)} %copy-done.5, f32[384]{0:T(512)S(1)} %copy-done.6, f32[192]{0:T(256)S(1)} %copy-done.7, f32[96]{0:T(128)S(1)} %copy-done.8, ...), custom_call_target="tpu_custom_call" | custom-call | tf_op jit(solution)/shard_map/tile/pallas_call | solution.py:306
  71.4 25.5 %all_to_all.10.got = f32[8,16,128]{2,1,0:T(8,128)S(1)} all-to-all(f32[8,16,128]{2,1,0:T(8,128)S(1)} %tile.1), channel_id=1, replica_groups=mesh['groups'=4,'ri'=8,'rj'=8] {'rj'}, dimensions={0} | all-to-all | bytes 131072 | tf_op jit(solution)/shard_map/all_to_all | solution.py:366
  96.9 0.8 rows.1
  (5 shorter events, 0.1 us)
Async XLA Ops:
  0.0 0.8 copy-start.4
  0.8 0.7 collective-permute-start
  2.2 28.8 %all-to-all-start = ((bf16[8,2,16,128]{3,2,1,0:T(8,128)(2,1)}), bf16[8,2,16,128]{3,2,1,0:T(8,128)(2,1)S(1)}, u32[]{:S(2)}, u32[]{:S(2)}) async-start(bf16[8,2,16,128]{3,2,1,0:T(8,128)(2,1)} %blocks.1), calls=%async_computation | async-start | bytes 131072 | tf_op jit(solution)/shard_map/all_to_all | solution.py:343
  31.0 12.3 %collective-permute-start.1 = (bf16[12,16,128]{2,1,0:T(8,128)(2,1)S(1)}, bf16[12,16,128]{2,1,0:T(8,128)(2,1)S(1)}, u32[]{:S(2)}, u32[]{:S(2)}) collective-permute-start(bf16[12,16,128]{2,1,0:T(8,128)(2,1)S(1)} %pad_maximum_fusion.refs_0_), channel_id=1, source_target_pairs={{0,0},{1,8},{2,16},{3,24},{4,32},{5,40},{6,48},{7,56},{8,1},{9,9},... | collective-permute-start | bytes 147464 | tf_op jit(solution)/shard_map/ppermute | solution.py:346
  33.9 3.3 %copy-start = (bf16[3,3,3,384,384]{4,3,2,1,0:T(8,128)(2,1)S(1)}, bf16[3,3,3,384,384]{4,3,2,1,0:T(8,128)(2,1)}, u32[]{:S(2)}) copy-start(bf16[3,3,3,384,384]{4,3,2,1,0:T(8,128)(2,1)} %param.13) | copy-start | bytes 23887876
  37.1 1.3 %copy-start.1 = (bf16[3,3,384,192]{2,3,1,0:T(8,128)(2,1)S(1)}, bf16[3,3,384,192]{2,3,1,0:T(8,128)(2,1)}, u32[]{:S(2)}) copy-start(bf16[3,3,384,192]{2,3,1,0:T(8,128)(2,1)} %param.15) | copy-start | bytes 3981316
  38.4 1.3 %copy-start.2 = (bf16[3,3,3,192,96]{4,3,2,1,0:T(8,128)(2,1)S(1)}, bf16[3,3,3,192,96]{4,3,2,1,0:T(8,128)(2,1)}, u32[]{:S(2)}) copy-start(bf16[3,3,3,192,96]{4,3,2,1,0:T(8,128)(2,1)} %refs_4_.2) | copy-start | bytes 2985988
  39.8 1.0 copy-start.3
  40.7 2.6 %copy-start.5 = (f32[384]{0:T(512)S(1)}, f32[384]{0:T(512)}, u32[]{:S(2)}) copy-start(f32[384]{0:T(512)} %refs_2_.1) | copy-start | bytes 4612
  40.7 2.6 %copy-start.6 = (f32[384]{0:T(512)S(1)}, f32[384]{0:T(512)}, u32[]{:S(2)}) copy-start(f32[384]{0:T(512)} %refs_3_.1) | copy-start | bytes 4612
  40.7 2.6 %copy-start.7 = (f32[192]{0:T(256)S(1)}, f32[192]{0:T(256)}, u32[]{:S(2)}) copy-start(f32[192]{0:T(256)} %refs_4_.3) | copy-start | bytes 2308
  40.7 2.6 %copy-start.8 = (f32[96]{0:T(128)S(1)}, f32[96]{0:T(128)}, u32[]{:S(2)}) copy-start(f32[96]{0:T(128)} %refs_5_.1) | copy-start | bytes 1156

commit v3 on v2

--- a/solution.py
+++ b/solution.py
@@ -11,7 +11,7 @@
 
 ROW = ("ri", "rj")
 EPS = 1e-06
-TILE_MIB = 36
+TILE_MIB = 40
 WEIGHTS_MIB = 8
 HALO = 4
 F32 = jnp.float32
@@ -21,16 +21,13 @@
 
 def weights_kernel(frames, dims, *refs):
     c_lat, c_hi, c_mid, c_lo = dims
-    (after, w_in, w_mid, w_up, w_low, w_out, wt, wmid, wc, wl, wo, win_v, wup_v, wlow_v, wout_v, sems) = refs
+    (after, w_in, w_up, w_low, w_out, wt, wc, wl, wo, win_v, wup_v, wlow_v, wout_v, sems) = refs
     copies = [
         pltpu.make_async_copy(w_in, win_v, sems.at[0]),
         pltpu.make_async_copy(w_up, wup_v, sems.at[1]),
         pltpu.make_async_copy(w_low, wlow_v, sems.at[2]),
         pltpu.make_async_copy(w_out, wout_v, sems.at[3]),
     ]
-    for a in range(3):
-        dst = wmid.at[:, (2 - a) * c_hi : (3 - a) * c_hi]
-        copies.append(pltpu.make_async_copy(w_mid.at[a], dst, sems.at[4 + a]))
     for copy in copies:
         copy.start()
 
@@ -79,17 +76,20 @@
     for ti in range(frames):
         for to in range(ti, min(frames, ti + 3)):
             wo[to * 32 : (to + 1) * 32, ti * 128 : ti * 128 + c_lo] = wout_v[ti - to + 2]
-    for copy in copies[4:]:
-        copy.wait()
 
 
 def tile_kernel(tr, tc, h, w, frames, dims, *refs):
     c_lat, c_hi, c_mid, c_lo = dims
-    (place, x, g1, g2, g3, g4, wt, wmid, wc, wl, wo, out,
-     xf, x9, first, act1, im, second, act2, third, act3, fourth, a4, zs) = refs
+    (place, x, g1, g2, g3, g4, w_mid, wt, wc, wl, wo, out,
+     xf, x9, first, act1, im, second, act2, third, act3, a4, zs, taps, sems) = refs
     s = tc + 2 * HALO
     r_first, r_mid, r_up, r_low = tr + 6, tr + 4, tr + 2, tr + 1
     row0, col0 = place[0], place[1]
+    copies = []
+    for a in range(3):
+        dst = taps.at[:, (2 - a) * c_hi : (3 - a) * c_hi]
+        copies.append(pltpu.make_async_copy(w_mid.at[a], dst, sems.at[a]))
+        copies[-1].start()
 
     def inside(rows, row_shift, col_shift):
         r = lax.broadcasted_iota(jnp.int32, (rows, s, 1), 0) + (row0 + row_shift)
@@ -135,13 +135,15 @@
     m2 = r_mid * s
     for t in range(frames):
         second[t] = first[t, s + 1 : s + 1 + m2, :]
+    for copy in copies:
+        copy.wait()
     for t in range(frames):
         for b in range(3):
             for e in range(3):
                 tap = 3 * b + e
                 im[t * m2 : (t + 1) * m2, tap * c_hi : (tap + 1) * c_hi] = act1[t, s * b + e : s * b + e + m2, :].astype(BF16)
         n = min(3, frames - t)
-        y = jnp.dot(im[t * m2 : (t + 1) * m2, :], wmid[:, : n * c_hi], preferred_element_type=F32)
+        y = jnp.dot(im[t * m2 : (t + 1) * m2, :], taps[:, : n * c_hi], preferred_element_type=F32)
         for d in range(n):
             second[t + d] += y[:, d * c_hi : (d + 1) * c_hi]
 
@@ -264,26 +266,26 @@
             out[t, o] = turned[32 * t + 9 * o : 32 * t + 9 * o + 2, :]
 
 
-def make_weights(after, w_in, w_mid, w_up, w_low, w_out, frames):
+def make_weights(after, w_in, w_up, w_low, w_out, frames):
     c_lat, c_hi = w_in.shape[-2:]
     c_mid, c_lo = w_low.shape[-2:]
     vmem = pl.BlockSpec(memory_space=pltpu.VMEM)
     anywhere = pl.BlockSpec(memory_space=pl.ANY)
     shapes = (
-        (9 * 128, frames * c_hi), (9 * c_hi, 3 * c_hi), (2, 2, 2, c_mid, 2 * c_hi), (18 * c_mid, 512), (128, frames * 128),
+        (9 * 128, frames * c_hi), (2, 2, 2, c_mid, 2 * c_hi), (18 * c_mid, 512), (128, frames * 128),
     )
     return pl.pallas_call(
         functools.partial(weights_kernel, frames, (c_lat, c_hi, c_mid, c_lo)),
         out_shape=[jax.ShapeDtypeStruct(shape, BF16) for shape in shapes],
-        in_specs=[anywhere] * 6,
-        out_specs=[vmem] * 5,
-        scratch_shapes=[pltpu.VMEM(v.shape, BF16) for v in (w_in, w_up, w_low, w_out)] + [pltpu.SemaphoreType.DMA((7,))],
+        in_specs=[anywhere] * 5,
+        out_specs=[vmem] * 4,
+        scratch_shapes=[pltpu.VMEM(v.shape, BF16) for v in (w_in, w_up, w_low, w_out)] + [pltpu.SemaphoreType.DMA((4,))],
         compiler_params=pltpu.CompilerParams(vmem_limit_bytes=WEIGHTS_MIB * 1024 * 1024),
         name="weights",
-    )(after, w_in, w_mid, w_up, w_low, w_out)
-
-
-def run_tile(place, x, g1, g2, g3, g4, weights, dims, tr, tc, h, w, frames):
+    )(after, w_in, w_up, w_low, w_out)
+
+
+def run_tile(place, x, g1, g2, g3, g4, w_mid, weights, dims, tr, tc, h, w, frames):
     c_lat, c_hi, c_mid, c_lo = dims
     s = tc + 2 * HALO
     m1, m2, m3 = (tr + 6) * s, (tr + 4) * s, (tr + 2) * s
@@ -299,19 +301,20 @@
         pltpu.VMEM((frames, m2 + 8, c_hi), F32),
         pltpu.VMEM((4, frames, m3, c_mid), F32),
         pltpu.VMEM((4, frames // 2, m3 + 16, 2 * c_mid), F32),
-        pltpu.VMEM((4, m4, frames * 128), F32),
         pltpu.VMEM((4, m4, frames * 128), BF16),
         pltpu.VMEM((4, m4 + 8, 128), F32),
+        pltpu.VMEM((9 * c_hi, 3 * c_hi), BF16),
+        pltpu.SemaphoreType.DMA((3,)),
     ]
     return pl.pallas_call(
         functools.partial(tile_kernel, tr, tc, h, w, frames, dims),
         out_shape=jax.ShapeDtypeStruct((tr, tc, 128), F32),
-        in_specs=[pl.BlockSpec(memory_space=pltpu.SMEM)] + [vmem] * 10,
+        in_specs=[pl.BlockSpec(memory_space=pltpu.SMEM)] + [vmem] * 5 + [pl.BlockSpec(memory_space=pl.ANY)] + [vmem] * 4,
         out_specs=vmem,
         scratch_shapes=scratch,
         compiler_params=pltpu.CompilerParams(vmem_limit_bytes=TILE_MIB * 1024 * 1024),
         name="tile",
-    )(place, x, g1, g2, g3, g4, *weights)
+    )(place, x, g1, g2, g3, g4, w_mid, *weights)
 
 
 def small_call(kernel, shape, dtype, scratch=(), name=None):
@@ -357,11 +360,12 @@
     colour = jnp.transpose(w_out, (0, 4, 1, 2, 3)).reshape(3, 9 * c_out, c_lo)
     colour = jnp.pad(colour, ((0, 0), (0, 32 - 9 * c_out), (0, 0)))
     weights = make_weights(
-        x[1], w_in, w_mid.reshape(3, -1, w_mid.shape[-1]), jnp.transpose(w_up, (0, 1, 3, 2)), w_low, colour, frames
+        x[1], w_in, jnp.transpose(w_up, (0, 1, 3, 2)), w_low, colour, frames
     )
     dims = w_in.shape[-2:] + w_low.shape[-2:]
     send = run_tile(
-        place, x[0], gain_one, gain_two, gain_three, gain_four, weights, dims, tr, tc, h, w, frames,
+        place, x[0], gain_one, gain_two, gain_three, gain_four, w_mid.reshape(3, -1, w_mid.shape[-1]),
+        weights, dims, tr, tc, h, w, frames,
     )
     got = lax.all_to_all(send, "rj", 0, 0, tiled=True)
     wide = [pltpu.VMEM((2 * w, 128), F32)]

time: 98.2 us -> 94.3 us (0.960)
  local copies, waits for them, and re-layouts: 8.45 us -> 5.21 us
  waiting for transfers between devices: 5.16 us -> 6.29 us
  blocking collectives: 25.5 us -> 24.4 us
    unnamed x18 -> x16, local copies, waits for them, and re-layouts: 7.64 us -> 4.41 us
    ppermute x1, waiting for transfers between devices: 0.01 us -> 1.13 us  [gather_tile(): return (lax.ppermute(pieces, ROW, swap), pieces)]
    all_to_all x1, blocking collectives: 25.5 us -> 24.4 us  [per_device(): got = lax.all_to_all(send, 'rj', 0, 0, tiled=True)]
  transfers between devices with their start and end apart: 3 -> 3, of which waited for: 1 -> 2; matrix products, arithmetic and copies ran while one was open for 1% -> 1% of each run, Pallas kernels for 3% -> 2%
where the time goes in v3:
time: 94.3 us; the launch traced here: 93.8 us
  Pallas kernels  31.4 us (33%)
  starting transfers between devices  26.3 us (28%)
  blocking collectives  24.4 us (26%)
  waiting for transfers between devices  6.29 us (7%)
  local copies, waits for them, and re-layouts  5.21 us (6%)
    pallas_call x1, Pallas kernels, run_tile(): pl.pallas_call(functools.partial(tile_kernel, tr, tc, h, w, frames, dims)...  28.2 us
    all_to_all x1, blocking collectives, per_device(): got = lax.all_to_all(send, 'rj', 0, 0, tiled=True)  24.4 us
    all_to_all x1, starting transfers between devices, gather_tile(): got = lax.all_to_all(blocks, 'rj', 0, 0, tiled=True)  23.7 us
    all_to_all x1, waiting for transfers between devices, gather_tile(): got = lax.all_to_all(blocks, 'rj', 0, 0, tiled=True)  5.16 us
    unnamed x16, local copies, waits for them, and re-layouts  4.41 us
    ppermute x1, starting transfers between devices, gather_tile(): return (lax.ppermute(pieces, ROW, swap), pieces)  1.95 us
  transfers between devices with their start and end apart: 3, of which 2 were waited for; matrix products, arithmetic and copies ran while one was open for 1% of the time, Pallas kernels for 2%

profile of v3, /device:TPU:37, one launch (start us, length us, event | category | flops | bytes accessed | tf_op | source)
XLA Modules:
  0.0 93.8 jit_solution(3865101371376797454)
XLA Ops:
  0.0 0.0 copy-start.6
  0.0 0.0 copy-start.7
  0.0 0.0 copy-start.3
  0.0 0.8 copy-done.3
  0.8 0.0 copy-start.4
  0.8 0.0 copy-start.5
  0.8 0.1 turn.1.mine
  0.9 0.7 collective-permute-start
  1.5 0.0 collective-permute-done.beside
  1.6 0.6 blocks.1
  2.2 23.7 %all-to-all-start = ((bf16[8,2,16,128]{3,2,1,0:T(8,128)(2,1)}), bf16[8,2,16,128]{3,2,1,0:T(8,128)(2,1)S(1)}, u32[]{:S(2)}, u32[]{:S(2)}) async-start(bf16[8,2,16,128]{3,2,1,0:T(8,128)(2,1)} %blocks.1), calls=%async_computation | async-start | bytes 131072 | tf_op jit(solution)/shard_map/all_to_all | solution.py:346
  25.9 5.2 %all-to-all-done = bf16[8,2,16,128]{3,2,1,0:T(8,128)(2,1)S(1)} async-done(((bf16[8,2,16,128]{3,2,1,0:T(8,128)(2,1)}), bf16[8,2,16,128]{3,2,1,0:T(8,128)(2,1)S(1)}, u32[]{:S(2)}, u32[]{:S(2)}) %all-to-all-start) | async-done | bytes 65568 | tf_op jit(solution)/shard_map/all_to_all | solution.py:346
  31.0 2.0 %collective-permute-start.1 = (bf16[12,16,128]{2,1,0:T(8,128)(2,1)S(1)}, bf16[12,16,128]{2,1,0:T(8,128)(2,1)S(1)}, u32[]{:S(2)}, u32[]{:S(2)}) collective-permute-start(bf16[12,16,128]{2,1,0:T(8,128)(2,1)S(1)} %pad_maximum_fusion.refs_0_), channel_id=1, source_target_pairs={{0,0},{1,8},{2,16},{3,24},{4,32},{5,40},{6,48},{7,56},{8,1},{9,9},... | collective-permute-start | bytes 147464 | tf_op jit(solution)/shard_map/ppermute | solution.py:349
  33.0 0.1 pad_add_fusion.refs_0_
  33.1 0.8 copy.16
  33.9 0.0 copy-start
  33.9 1.3 %copy-done = bf16[3,3,384,192]{2,3,1,0:T(8,128)(2,1)S(1)} copy-done((bf16[3,3,384,192]{2,3,1,0:T(8,128)(2,1)S(1)}, bf16[3,3,384,192]{2,3,1,0:T(8,128)(2,1)}, u32[]{:S(2)}) %copy-start) | copy-done | bytes 1327128
  35.2 0.0 copy-start.1
  35.2 1.3 %copy-done.1 = bf16[3,3,3,192,96]{4,3,2,1,0:T(8,128)(2,1)S(1)} copy-done((bf16[3,3,3,192,96]{4,3,2,1,0:T(8,128)(2,1)S(1)}, bf16[3,3,3,192,96]{4,3,2,1,0:T(8,128)(2,1)}, u32[]{:S(2)}) %copy-start.1) | copy-done | bytes 995352
  36.5 0.0 copy-start.2
  36.5 1.0 %copy-done.2 = bf16[3,3,3,16,384]{4,3,2,1,0:T(8,128)(2,1)S(1)} copy-done((bf16[3,3,3,16,384]{4,3,2,1,0:T(8,128)(2,1)S(1)}, bf16[3,3,3,16,384]{4,3,2,1,0:T(8,128)(2,1)}, u32[]{:S(2)}) %copy-start.2) | copy-done | bytes 331800
  37.5 1.7 %weights.1 = (bf16[1152,1536]{1,0:T(8,128)(2,1)S(1)}, bf16[2,2,2,192,768]{4,3,2,1,0:T(8,128)(2,1)S(1)}, bf16[3456,512]{1,0:T(8,128)(2,1)S(1)}, bf16[128,512]{1,0:T(8,128)(2,1)S(1)}) custom-call(bf16[12,16,128]{2,1,0:T(8,128)(2,1)S(1)} %pad_maximum_fusion.refs_0_, bf16[3,3,3,16,384]{4,3,2,1,0:T(8,128)(2,1)S(1)} %copy-done.2, ...), custom_call_target="tpu_custom_call" | custom-call | tf_op jit(solution)/shard_map/weights/pallas_call | solution.py:277
  39.3 1.1 %collective-permute-done.1.refs_1_ = bf16[12,16,128]{2,1,0:T(8,128)(2,1)S(1)} collective-permute-done((bf16[12,16,128]{2,1,0:T(8,128)(2,1)S(1)}, bf16[12,16,128]{2,1,0:T(8,128)(2,1)S(1)}, u32[]{:S(2)}, u32[]{:S(2)}) %collective-permute-start.1) | collective-permute-done | bytes 49184 | tf_op jit(solution)/shard_map/ppermute | solution.py:349
  40.4 0.0 copy-done.6
  40.4 0.0 copy-done.7
  40.4 0.0 copy-done.4
  40.4 0.0 copy-done.5
  40.4 28.2 %tile.1 = f32[8,16,128]{2,1,0:T(8,128)S(1)} custom-call(s32[2]{0:T(128)S(1)} %pad_add_fusion.refs_0_, bf16[12,16,128]{2,1,0:T(8,128)(2,1)S(1)} %collective-permute-done.1.refs_1_, f32[384]{0:T(512)S(1)} %copy-done.4, f32[384]{0:T(512)S(1)} %copy-done.5, f32[192]{0:T(256)S(1)} %copy-done.6, f32[96]{0:T(128)S(1)} %copy-done.7, bf16[3,3456,384]{2,1,0:T(8,128)(2,1)} %bitcast.22, ...), custom_call_target="tpu_custom_call" | custom-call | tf_op jit(solution)/shard_map/tile/pallas_call | solution.py:309
  68.6 24.4 %all_to_all.10.got = f32[8,16,128]{2,1,0:T(8,128)S(1)} all-to-all(f32[8,16,128]{2,1,0:T(8,128)S(1)} %tile.1), channel_id=1, replica_groups=mesh['groups'=4,'ri'=8,'rj'=8] {'rj'}, dimensions={0} | all-to-all | bytes 131072 | tf_op jit(solution)/shard_map/all_to_all | solution.py:370
  93.0 0.8 rows.1
  (5 shorter events, 0.1 us)
Async XLA Ops:
  0.0 40.4 %copy-start.6 = (f32[192]{0:T(256)S(1)}, f32[192]{0:T(256)}, u32[]{:S(2)}) copy-start(f32[192]{0:T(256)} %refs_4_.1) | copy-start | bytes 2308
  0.0 40.4 %copy-start.7 = (f32[96]{0:T(128)S(1)}, f32[96]{0:T(128)}, u32[]{:S(2)}) copy-start(f32[96]{0:T(128)} %refs_5_.1) | copy-start | bytes 1156
  0.0 0.8 copy-start.3
  0.8 39.6 %copy-start.4 = (f32[384]{0:T(512)S(1)}, f32[384]{0:T(512)}, u32[]{:S(2)}) copy-start(f32[384]{0:T(512)} %refs_2_.1) | copy-start | bytes 4612
  0.8 39.6 %copy-start.5 = (f32[384]{0:T(512)S(1)}, f32[384]{0:T(512)}, u32[]{:S(2)}) copy-start(f32[384]{0:T(512)} %refs_3_.3) | copy-start | bytes 4612
  0.9 0.7 collective-permute-start
  2.2 28.8 %all-to-all-start = ((bf16[8,2,16,128]{3,2,1,0:T(8,128)(2,1)}), bf16[8,2,16,128]{3,2,1,0:T(8,128)(2,1)S(1)}, u32[]{:S(2)}, u32[]{:S(2)}) async-start(bf16[8,2,16,128]{3,2,1,0:T(8,128)(2,1)} %blocks.1), calls=%async_computation | async-start | bytes 131072 | tf_op jit(solution)/shard_map/all_to_all | solution.py:346
  31.0 9.3 %collective-permute-start.1 = (bf16[12,16,128]{2,1,0:T(8,128)(2,1)S(1)}, bf16[12,16,128]{2,1,0:T(8,128)(2,1)S(1)}, u32[]{:S(2)}, u32[]{:S(2)}) collective-permute-start(bf16[12,16,128]{2,1,0:T(8,128)(2,1)S(1)} %pad_maximum_fusion.refs_0_), channel_id=1, source_target_pairs={{0,0},{1,8},{2,16},{3,24},{4,32},{5,40},{6,48},{7,56},{8,1},{9,9},... | collective-permute-start | bytes 147464 | tf_op jit(solution)/shard_map/ppermute | solution.py:349
  33.9 1.3 %copy-start = (bf16[3,3,384,192]{2,3,1,0:T(8,128)(2,1)S(1)}, bf16[3,3,384,192]{2,3,1,0:T(8,128)(2,1)}, u32[]{:S(2)}) copy-start(bf16[3,3,384,192]{2,3,1,0:T(8,128)(2,1)} %param.15) | copy-start | bytes 3981316
  35.2 1.3 %copy-start.1 = (bf16[3,3,3,192,96]{4,3,2,1,0:T(8,128)(2,1)S(1)}, bf16[3,3,3,192,96]{4,3,2,1,0:T(8,128)(2,1)}, u32[]{:S(2)}) copy-start(bf16[3,3,3,192,96]{4,3,2,1,0:T(8,128)(2,1)} %refs_3_.2) | copy-start | bytes 2985988
  36.5 1.0 %copy-start.2 = (bf16[3,3,3,16,384]{4,3,2,1,0:T(8,128)(2,1)S(1)}, bf16[3,3,3,16,384]{4,3,2,1,0:T(8,128)(2,1)}, u32[]{:S(2)}) copy-start(bf16[3,3,3,16,384]{4,3,2,1,0:T(8,128)(2,1)} %refs_1_.1) | copy-start | bytes 995332
